TPU v7x, 8 devices: a whole 2x2x1 slice. The times are simulated.
8 devices in a mesh: dp: 1 (over z), tp: 2 (over y), sp: 4 (over x, core).
Axes of the slice: x: 2, y: 2, z: 1, core: 2. Of those that a mesh axis runs over, the one named last changes fastest.
Arguments:
- hidden: bfloat16 [64, 4096], P('dp')
- norm_scale: bfloat16 [4096], replicated
- w_qkv: bfloat16 [4096, 6144], P(None, 'tp')
- w_out: bfloat16 [4096, 4096], P('tp')
- k_cache: bfloat16 [64, 512, 8, 128], P('dp', 'sp', 'tp')
- v_cache: bfloat16 [64, 512, 8, 128], P('dp', 'sp', 'tp')
- positions: int32 [64], P('dp')
Outputs:
- output 1: bfloat16 [64, 4096], P('dp')
- output 2: bfloat16 [64, 512, 8, 128], P('dp', 'sp', 'tp')
- output 3: bfloat16 [64, 512, 8, 128], P('dp', 'sp', 'tp')
All inputs are finite; a program needn't handle non-finite values.
Results may differ from a plain program's by a relative error of at most 0.00736725.
Values sent between devices are 32-bit elements.
A program may use at most 1 GiB of HBM per device.

v0:
```python
import math
import jax
import jax.numpy as jnp
from jax import lax
from jax.sharding import PartitionSpec as P


def rope_apply(head_vals, positions):
    half_dim = head_vals.shape[-1] // 2
    inv_freq = jnp.exp(jnp.arange(half_dim, dtype=jnp.float32) * (-2.0 * math.log(500000.0) / head_vals.shape[-1]))
    angles = positions.astype(jnp.float32)[:, None] * inv_freq[None, :]
    cos_part = jnp.cos(angles)[:, None, None, :]
    sin_part = jnp.sin(angles)[:, None, None, :]
    first_half = head_vals[..., :half_dim]
    second_half = head_vals[..., half_dim:]
    return jnp.concatenate([first_half * cos_part - second_half * sin_part, second_half * cos_part + first_half * sin_part], axis=-1)


def layer_norm_bf16(hidden_f32, norm_scale):
    row_mean = jnp.mean(hidden_f32, axis=-1, keepdims=True)
    centered = hidden_f32 - row_mean
    row_var = jnp.mean(centered * centered, axis=-1, keepdims=True)
    return (centered * lax.rsqrt(row_var + 1e-5) * norm_scale.astype(jnp.float32)).astype(jnp.bfloat16)


def solution(mesh):
    cache_spec = P('dp', 'sp', 'tp', None)

    def local_step(hidden, norm_scale, w_qkv, w_out, k_cache, v_cache, positions):
        n_seq, seq_local, kv_local, head_dim = k_cache.shape
        q_per_kv = w_qkv.shape[1] // (kv_local * head_dim) - 2
        hidden_f32 = hidden.astype(jnp.float32)
        normed = layer_norm_bf16(hidden_f32, norm_scale)
        qkv_proj = jnp.clip(jnp.dot(normed, w_qkv, preferred_element_type=jnp.float32).astype(jnp.bfloat16), -8.0, 8.0)
        grouped = qkv_proj.reshape(n_seq, kv_local, q_per_kv + 2, head_dim)
        rotated = rope_apply(grouped[:, :, : q_per_kv + 1].astype(jnp.float32), positions).astype(jnp.bfloat16)
        queries = rotated[:, :, :q_per_kv]
        row_index = lax.axis_index('sp') * seq_local + jnp.arange(seq_local)
        new_row = (row_index[None, :] == positions[:, None])[:, :, None, None]
        k_upd = jnp.where(new_row, rotated[:, :, q_per_kv][:, None], k_cache)
        v_upd = jnp.where(new_row, grouped[:, :, q_per_kv + 1][:, None], v_cache)
        scores = jnp.einsum('bgqd,bsgd->bgqs', queries, k_upd, preferred_element_type=jnp.float32) * (head_dim ** -0.5)
        valid_mask = row_index[None, :] <= positions[:, None]
        scores = jnp.where(valid_mask[:, None, None, :], scores, -1e30)
        local_max = jnp.max(scores, axis=-1)
        weights = jnp.exp(scores - local_max[..., None])
        local_sum = jnp.sum(weights, axis=-1)
        local_out = jnp.einsum('bgqs,bsgd->bgqd', weights.astype(jnp.bfloat16), v_upd, preferred_element_type=jnp.float32)
        global_max = lax.pmax(local_max, 'sp')
        factor = jnp.exp(local_max - global_max)
        packed = jnp.concatenate([local_out * factor[..., None], (local_sum * factor)[..., None]], axis=-1)
        merged = lax.psum(packed, 'sp')
        attn_out = merged[..., :head_dim] / merged[..., head_dim:]
        attn_flat = attn_out.reshape(n_seq, kv_local * q_per_kv * head_dim).astype(jnp.bfloat16)
        head_part = jnp.dot(attn_flat, w_out, preferred_element_type=jnp.float32)
        proj_sum = lax.psum(head_part, 'tp')
        h_out = (hidden_f32 + proj_sum).astype(jnp.bfloat16)
        return h_out, k_upd, v_upd

    return jax.shard_map(
        local_step,
        mesh=mesh,
        in_specs=(P('dp', None), P(None), P(None, 'tp'), P('tp', None), cache_spec, cache_spec, P('dp')),
        out_specs=(P('dp', None), cache_spec, cache_spec),
        check_vma=False,
    )
```

profile of v0, /device:TPU:0, one launch (start us, length us, event | category | flops | bytes accessed | tf_op | source)
XLA Modules:
  0.0 161.1 jit_solution(7422554771954445428)
XLA Ops:
  7.2 0.0 all-reduce.3.cloned.1.call-start
  7.2 1.2 convert_reduce_fusion
  8.5 1.3 fusion.16
  9.8 0.7 convert_element_type.36
  10.5 0.0 copy-start.2
  10.5 12.9 %fusion.4 = bf16[64,3072]{1,0:T(8,128)(2,1)S(1)} fusion(bf16[4096,3072]{1,0:T(8,128)(2,1)} %param.9, bf16[64,4096]{1,0:T(8,128)(2,1)} %param.7, f32[4096]{0:T(1024)S(1)} %convert_element_type.36, f32[64]{0:T(128)S(1)} %add_rsqrt_fusion, f32[64]{0:T(128)S(1)} %broadcast_multiply_fusion), kind=kOutput, calls=%fused_computation.7 | convolution fusion | flops 1612316672 | bytes 26100224 | tf_op jit(solution)/shard_map/dot_general | solution.py:34
  23.5 0.5 reshape.131
  23.9 0.1 slice.37
  24.1 0.1 slice_convert_fusion
  24.3 0.0 copy-done.2
  24.3 0.1 broadcast_compare_fusion.1
  24.4 0.1 copy.27
  24.4 0.2 multiply_cosine_fusion
  24.6 0.5 subtract_convert_fusion
  25.2 0.5 pad_maximum_fusion.1
  25.7 0.1 copy.24
  25.8 13.8 %broadcast_select_fusion = (bf16[64,128,4,128]{3,2,1,0:T(4,128)(2,1)}, bf16[64,128,4,128]{3,2,1,0:T(4,128)(2,1)S(1)}) fusion(bf16[64,128,4,128]{3,2,1,0:T(4,128)(2,1)} %param.12, pred[64,128]{1,0:T(8,128)(4,1)S(1)} %get-tuple-element.10, bf16[64,4,128]{2,1,0:T(4,128)(2,1)S(1)} %copy.27, bf16[64,128,4,128]{3,2,1,0:T(4,128)(2,1)} %param.11, ...), kind=kLoop, calls=%fused_computation.4 | loop fusion | flops 8388608 | bytes 33693696 | tf_op jit(solution)/shard_map/jit(_where)/select_n | solution.py:41
  39.5 0.0 copy-start.1
  39.6 3.4 %copy-done.1 = bf16[64,128,4,128]{3,2,1,0:T(4,128)(2,1)} copy-done((bf16[64,128,4,128]{3,2,1,0:T(4,128)(2,1)}, bf16[64,128,4,128]{3,2,1,0:T(4,128)(2,1)S(1)}, u32[]{:S(2)}) %copy-start.1) | copy-done | bytes 8388632
  42.9 4.7 %fusion.32 = (f32[64,4,4]{2,1,0:T(4,128)S(1)}, f32[64,4,4,128]{3,2,1,0:T(4,128)S(1)}) fusion(bf16[64,128,4,128]{3,2,1,0:T(4,128)(2,1)S(1)} %get-tuple-element.8, bf16[64,4,5,64]{3,2,1,0:T(8,128)(2,1)S(1)} %get-tuple-element.5, bf16[64,4,5,64]{3,2,1,0:T(8,128)(2,1)S(1)} %get-tuple-element.6, pred[64,128]{1,0:T(8,128)(4,1)S(1)} %get-tuple-element.9), kind=kOutput, calls=%fused_computation.50 | convolution fusion | flops 34470912 | bytes 9252864 | tf_op jit(solution)/shard_map/bgqd,bsgd->bgqs/dot_general | solution.py:42
  47.7 15.0 %pmax.7 = f32[64,4,4]{2,1,0:T(4,128)S(1)} all-reduce(f32[64,4,4]{2,1,0:T(4,128)S(1)} %get-tuple-element.13), channel_id=1, replica_groups=mesh['dp'=1,'tp'=2,'sp'=4] {'sp'}, use_global_device_ids=true, to_apply=%region_3.4 | all-reduce | flops 1024 | bytes 8192 | tf_op jit(solution)/shard_map/pmax | solution.py:49
  62.7 0.7 fusion.25
  63.4 0.1 multiply_bitcast_fusion
  63.5 1.7 %copy.30 = f32[64,4,4,1]{3,2,1,0:T(4,128)S(1)} copy(f32[64,4,4,1]{2,1,0,3:T(4,128)S(1)} %get-tuple-element.3) | data formatting | bytes 8192 | tf_op jit(solution)/shard_map/broadcast_in_dim | solution.py:51
  65.2 5.7 %fusion.10 = f32[64,4,4,128]{3,2,1,0:T(4,128)S(1)} fusion(bf16[64,128,4,128]{3,2,1,0:T(4,128)(2,1)} %get-tuple-element.7, f32[64,4,4,128]{3,2,1,0:T(4,128)S(1)} %get-tuple-element.14, f32[64,4,4]{2,1,0:T(4,128)S(1)} %get-tuple-element.4, f32[64,4,4]{2,1,0:T(4,128)S(1)} %get-tuple-element.13), kind=kOutput, calls=%fused_computation.14 | convolution fusion | flops 33947648 | bytes 9445376 | tf_op jit(solution)/shard_map/bgqs,bsgd->bgqd/dot_general | solution.py:48
  70.9 1.3 pad_maximum_fusion
  72.2 0.0 all-reduce.3.cloned.1.call-update
  72.2 0.0 all-reduce.5.cloned.1.call-start
  72.3 31.0 %all-reduce.3.cloned.1.call-done = f32[64,4,4,129]{3,2,1,0:T(4,128)} async-done(((f32[64,4,4,129]{3,2,1,0:T(4,128)}), f32[64,4,4,129]{3,2,1,0:T(4,128)}) %all-reduce.3.cloned.1.call-update) | async-done | bytes 528400 | tf_op jit(solution)/shard_map/psum | solution.py:52
  103.3 1.1 slice.39
  104.4 1.6 %copy.35 = f32[64,4,4,1]{2,1,0,3:T(4,128)S(1)} copy(f32[64,4,4,1]{3,2,1,0:T(4,128)S(1)} %slice.39) | data formatting | bytes 8192 | tf_op jit(solution)/shard_map/div | solution.py:53
  106.0 1.4 fusion.24
  107.4 0.2 convert_element_type.43
  107.6 0.0 copy-start
  107.6 9.9 %fusion.33 = f32[64,4096]{1,0:T(8,128)} fusion(bf16[64,2048]{1,0:T(8,128)(2,1)S(1)} %convert_element_type.43, bf16[2048,4096]{1,0:T(8,128)(2,1)} %param.10), kind=kOutput, calls=%fused_computation.51 | convolution fusion | flops 1073741824 | bytes 18087936 | tf_op jit(solution)/shard_map/dot_general | solution.py:55
  117.5 0.0 all-reduce.5.cloned.1.call-update
  117.5 34.7 %all-reduce.5.cloned.1.call-done = f32[64,4096]{1,0:T(8,128)} async-done(((f32[64,4096]{1,0:T(8,128)}), f32[64,4096]{1,0:T(8,128)}) %all-reduce.5.cloned.1.call-update) | async-done | bytes 1048592 | tf_op jit(solution)/shard_map/psum | solution.py:56
  152.2 0.0 copy-done
  152.2 2.1 %fusion.19 = bf16[64,4096]{1,0:T(8,128)(2,1)} fusion(f32[64,4096]{1,0:T(8,128)} %all-reduce.5.cloned.1.call-done, bf16[64,4096]{1,0:T(8,128)(2,1)S(1)} %copy-done), kind=kLoop, calls=%fused_computation.19 | loop fusion | flops 786432 | bytes 2097152 | tf_op jit(solution)/shard_map/convert_element_type | solution.py:57
  (7 shorter events, 0.1 us)
Async XLA Ops:
  7.2 96.1 %all-reduce.3.cloned.1.call-start = ((), (), s32[]{:S(2)}) async-start(), calls=%async_computation | async-start | bytes 2097152 | tf_op jit(solution)/shard_map/psum | solution.py:52
  10.5 13.7 %copy-start.2 = (s32[64]{0:T(128)S(1)}, s32[64]{0:T(128)}, u32[]{:S(2)}) copy-start(s32[64]{0:T(128)} %param.13) | copy-start | bytes 772
  39.5 3.4 %copy-start.1 = (bf16[64,128,4,128]{3,2,1,0:T(4,128)(2,1)}, bf16[64,128,4,128]{3,2,1,0:T(4,128)(2,1)S(1)}, u32[]{:S(2)}) copy-start(bf16[64,128,4,128]{3,2,1,0:T(4,128)(2,1)S(1)} %get-tuple-element.8) | copy-start | bytes 25165828
  72.2 80.0 %all-reduce.5.cloned.1.call-start = ((), (), s32[]{:S(2)}) async-start(), calls=%async_computation.1 | async-start | bytes 2097152 | tf_op jit(solution)/shard_map/psum | solution.py:56
  107.6 44.6 %copy-start = (bf16[64,4096]{1,0:T(8,128)(2,1)S(1)}, bf16[64,4096]{1,0:T(8,128)(2,1)}, u32[]{:S(2)}) copy-start(bf16[64,4096]{1,0:T(8,128)(2,1)} %param.7) | copy-start | bytes 1572868
Sparse Core Ops, SparseCore 0:
  72.4 30.8 all-reduce.2
  117.6 34.5 all-reduce.4
where the time goes:
time: 162 us; the launch traced here: 161 us
  waiting for transfers between devices  65.7 us (41%)
  matrix products  33.2 us (20%)
  other arithmetic  24.1 us (15%)
  blocking collectives  15 us (9%)
  between operations  14.2 us (9%)
  local copies, waits for them, and re-layouts  8.72 us (5%)
    psum x1, waiting for transfers between devices, local_step(): proj_sum = lax.psum(head_part, 'tp')  34.7 us
    psum x1, waiting for transfers between devices, local_step(): merged = lax.psum(packed, 'sp')  31 us
    pmax x1, blocking collectives, local_step(): global_max = lax.pmax(local_max, 'sp')  15 us
    select_n x1, other arithmetic, local_step(): v_upd = jnp.where(new_row, grouped[:, :, q_per_kv + 1][:, None], v_cache)  13.8 us
    dot_general x1, matrix products, local_step(): jnp.dot(normed, w_qkv, preferred_element_type=jnp.float32)  12.9 us
    dot_general x1, matrix products, local_step(): head_part = jnp.dot(attn_flat, w_out, preferred_element_type=jnp.float32)  9.88 us
    dot_general x1, matrix products, local_step(): jnp.einsum('bgqs,bsgd->bgqd', weights.astype(jnp.bfloat16), v_upd, prefer...  5.72 us
    dot_general x1, matrix products, local_step(): jnp.einsum('bgqd,bsgd->bgqs', queries, k_upd, preferred_element_type=jnp....  4.72 us
  transfers between devices with their start and end apart: 2, of which 2 were waited for; matrix products, arithmetic and copies ran while one was open for 0% of the time, Pallas kernels for 0%

commit v1 on v0

v1 whole, which is shorter than its diff:
```python
import functools
import math

import jax
import jax.numpy as jnp
from jax import lax
from jax.experimental import pallas as pl
from jax.experimental.pallas import tpu as pltpu
from jax.sharding import PartitionSpec as P

MESH = pl.DeviceIdType.MESH
NEG = -1e30
UNROLL = 4
W_PARTS = 2
CACHE_PARTS = 8
OUT_CHUNKS = 4
LN_EPS = 1e-5


def attention_kernel(pos_ref, h_ref, scale_ref, w_ref, kc_ref, vc_ref,
                     ko_ref, vo_ref, o_ref, ml_ref,
                     k_ref, v_ref, w_buf, u_ref, q_ref, kn_ref, vn_ref, ang_ref, idx_ref,
                     w_sem, k_sem, v_sem, ko_sem, vo_sem):
    n_seq, d_model = h_ref.shape
    rows = k_ref.shape[1]
    head = k_ref.shape[2]
    kv_local = w_ref.shape[1] // (6 * head)
    group_cols = 6 * head
    base = lax.axis_index('sp') * (rows // kv_local)

    w_rows = d_model // W_PARTS
    c_rows = n_seq // CACHE_PARTS

    def w_copy(g, part):
        at = pl.ds(part * w_rows, w_rows)
        return pltpu.make_async_copy(
            w_ref.at[at, pl.ds(g * group_cols, group_cols)], w_buf.at[g, at], w_sem.at[g, part])

    def c_copies(i):
        at = pl.ds(i * c_rows, c_rows)
        return (pltpu.make_async_copy(kc_ref.at[at], k_ref.at[at], k_sem.at[i]),
                pltpu.make_async_copy(vc_ref.at[at], v_ref.at[at], v_sem.at[i]))

    def out_copies(i):
        at = pl.ds(i * c_rows, c_rows)
        return (pltpu.make_async_copy(k_ref.at[at], ko_ref.at[at], ko_sem.at[i]),
                pltpu.make_async_copy(v_ref.at[at], vo_ref.at[at], vo_sem.at[i]))

    for g in range(kv_local):
        for part in range(W_PARTS):
            w_copy(g, part).start()

    blocks = d_model // 128
    total = jnp.zeros((n_seq, 128), jnp.float32)
    for i in range(blocks):
        total += h_ref[:, i * 128:(i + 1) * 128].astype(jnp.float32)
    mean = jnp.sum(total, axis=1, keepdims=True) * (1.0 / d_model)
    total = jnp.zeros((n_seq, 128), jnp.float32)
    for i in range(blocks):
        cen = h_ref[:, i * 128:(i + 1) * 128].astype(jnp.float32) - mean
        total += cen * cen
    var = jnp.sum(total, axis=1, keepdims=True) * (1.0 / d_model)
    rstd = lax.rsqrt(var + LN_EPS)
    for i in range(blocks):
        cen = h_ref[:, i * 128:(i + 1) * 128].astype(jnp.float32) - mean
        u_ref[:, i * 128:(i + 1) * 128] = (
            cen * rstd * scale_ref[i:i + 1, :].astype(jnp.float32)).astype(jnp.bfloat16)

    lane = lax.broadcasted_iota(jnp.int32, (1, head), 1)
    half = head // 2
    inv_freq = jnp.exp((lane % half).astype(jnp.float32) * (-2.0 * math.log(500000.0) / head))

    def fill(b, _):
        ang_ref[pl.ds(b, 1), :] = jnp.full((1, head), pos_ref[b].astype(jnp.float32)) * inv_freq
        return 0
    lax.fori_loop(0, n_seq, fill, 0)
    cos = jnp.cos(ang_ref[...])
    sin = jnp.sin(ang_ref[...]) * jnp.where(lane < half, -1.0, 1.0)

    def rope(x):
        return (x * cos + pltpu.roll(x, half, 1) * sin).astype(jnp.bfloat16).astype(jnp.float32)

    n_q = 4 * kv_local
    col = lax.broadcasted_iota(jnp.int32, (n_q, rows), 1)
    qg = lax.broadcasted_iota(jnp.int32, (n_q, rows), 0) // 4
    idx_ref[...] = jnp.where(col % kv_local == qg, col // kv_local, 1 << 20)

    started = 0
    for g in range(kv_local):
        acc = jnp.zeros((n_seq, group_cols), jnp.float32)
        for part in range(W_PARTS):
            w_copy(g, part).wait()
            if started < CACHE_PARTS:
                for c in c_copies(started):
                    c.start()
                started += 1
            at = pl.ds(part * w_rows, w_rows)
            acc += jnp.dot(u_ref[:, at], w_buf[g, at, :], preferred_element_type=jnp.float32)
        qkv = jnp.clip(acc.astype(jnp.bfloat16).astype(jnp.float32), -8.0, 8.0)
        for j in range(4):
            q_ref[:, g * 4 + j, :] = rope(qkv[:, j * head:(j + 1) * head])
        kn = rope(qkv[:, 4 * head:5 * head])
        vn = qkv[:, 5 * head:]
        for r in range(16 // kv_local):
            kn_ref[:, r * kv_local + g, :] = kn
            vn_ref[:, r * kv_local + g, :] = vn
    for i in range(started, CACHE_PARTS):
        for c in c_copies(i):
            c.start()

    scale = head ** -0.5
    per = 16 // kv_local
    row16 = lax.broadcasted_iota(jnp.int32, (16, head), 0) // kv_local
    lane_id = lax.broadcasted_iota(jnp.int32, (n_q, 128), 1)

    def insert(b):
        p = pos_ref[b] - base

        @pl.when((p >= 0) & (p < rows // kv_local))
        def _():
            at = pl.ds(pl.multiple_of((p // per) * 16, 16), 16)
            hit = row16 == p % per
            k_ref[b, at, :] = jnp.where(hit, kn_ref[b], k_ref[b, at, :].astype(jnp.float32)).astype(jnp.bfloat16)
            v_ref[b, at, :] = jnp.where(hit, vn_ref[b], v_ref[b, at, :].astype(jnp.float32)).astype(jnp.bfloat16)

    def attend(b, m_all, l_all):
        p = pos_ref[b] - base
        s = lax.dot_general(q_ref[b].astype(jnp.bfloat16), k_ref[b], (((1,), (1,)), ((), ())),
                            preferred_element_type=jnp.float32)
        s = jnp.where(idx_ref[...] <= p, s * scale, NEG)
        m = jnp.max(s, axis=1, keepdims=True)
        e = jnp.exp(s - m)
        l = jnp.sum(e, axis=1, keepdims=True)
        o_ref[b] = jnp.dot(e.astype(jnp.bfloat16), v_ref[b], preferred_element_type=jnp.float32)
        return jnp.where(lane_id == b, m, m_all), jnp.where(lane_id == b, l, l_all)

    m_all = jnp.zeros((n_q, 128), jnp.float32)
    l_all = jnp.zeros((n_q, 128), jnp.float32)
    for i in range(CACHE_PARTS):
        for c in c_copies(i):
            c.wait()

        def step(t, carry):
            b0 = i * c_rows + t * UNROLL
            for k in range(UNROLL):
                insert(b0 + k)
            for k in range(UNROLL):
                carry = attend(b0 + k, *carry)
            return carry
        m_all, l_all = lax.fori_loop(0, c_rows // UNROLL, step, (m_all, l_all))
        for c in out_copies(i):
            c.start()
    ml_ref[0:n_q, :] = m_all
    ml_ref[n_q:, :] = l_all
    for i in range(CACHE_PARTS):
        for c in out_copies(i):
            c.wait()


def finish_kernel(h_ref, w_ref, o_ref, ml_ref, out_ref,
                  w_buf, sib_o, mine_o, sib_ml, send_o, send_ml, x_o, x_ml, att, att_send, lhs,
                  part, y_in, fin, x_in, d_in, d_in2,
                  w_sem, s_sem, r_sem, ys_sem, yr_sem, xs_sem, xr_sem, ds_sem, dr_sem, es_sem, er_sem):
    n_q = ml_ref.shape[0] // 2
    sp = lax.axis_index('sp')
    tp = lax.axis_index('tp')
    x, c = sp // 2, sp % 2
    sib = {'sp': x * 2 + (1 - c)}
    xn = {'sp': (1 - x) * 2 + c}
    yn = {'tp': 1 - tp}

    half_cols = w_buf.shape[1]
    cc = half_cols // OUT_CHUNKS
    q4 = sib_o.shape[0]
    own_col = c * half_cols
    oth_col = (1 - c) * half_cols

    def w_copy(j):
        return pltpu.make_async_copy(
            w_ref.at[:, pl.ds(pl.multiple_of(own_col + j * cc, 128), cc)],
            w_buf.at[:, pl.ds(j * cc, cc)], w_sem.at[j])

    for j in range(OUT_CHUNKS):
        w_copy(j).start()

    barrier = pltpu.get_barrier_semaphore()
    for dev in (sib, xn, yn):
        pl.semaphore_signal(barrier, inc=1, device_id=dev, device_id_type=MESH)
    pl.semaphore_wait(barrier, 3)

    def remote(src, dst, ssem, rsem, dev):
        return pltpu.make_async_remote_copy(src_ref=src, dst_ref=dst, send_sem=ssem, recv_sem=rsem,
                                            device_id=dev, device_id_type=MESH)

    def quarter(xx, k):
        return pl.ds(xx * (2 * q4) + k * q4, q4)

    c_ml = remote(ml_ref, sib_ml, s_sem.at[0], r_sem.at[0], sib)
    c_sib = remote(o_ref.at[quarter(1 - x, 1 - c)], sib_o, s_sem.at[1], r_sem.at[1], sib)
    c_mine = remote(o_ref.at[quarter(x, 1 - c)], mine_o, s_sem.at[2], r_sem.at[2], sib)
    c_ml.start()
    c_sib.start()
    c_mine.start()

    c_ml.wait_recv()
    m0, l0 = ml_ref[:n_q], ml_ref[n_q:]
    m1, l1 = sib_ml[:n_q], sib_ml[n_q:]
    m = jnp.maximum(m0, m1)
    f0, f1 = jnp.exp(m0 - m), jnp.exp(m1 - m)
    l = l0 * f0 + l1 * f1
    send_ml[:n_q] = m
    send_ml[n_q:] = l
    c_xml = remote(send_ml, x_ml, s_sem.at[3], r_sem.at[3], xn)
    c_xml.start()

    def column(a, xx, k, i):
        v = None
        for dx in range(2):
            for dk in range(2):
                at = dx * 2 * q4 + dk * q4 + i
                piece = jnp.broadcast_to(a[:, at:at + 1], (n_q, 128))
                pick = (xx == dx) & (k == dk)
                v = piece if v is None else jnp.where(pick, piece, v)
        return v

    c_sib.wait_recv()
    for i in range(q4):
        at = (1 - x) * (2 * q4) + c * q4 + i
        send_o[i] = (o_ref[at] * column(f0, 1 - x, c, i) + sib_o[i] * column(f1, 1 - x, c, i))
    c_xo = remote(send_o, x_o, s_sem.at[4], r_sem.at[4], xn)
    c_xo.start()

    c_xml.wait_recv()
    m2, l2 = x_ml[:n_q], x_ml[n_q:]
    mm = jnp.maximum(m, m2)
    g, g2 = jnp.exp(m - mm), jnp.exp(m2 - mm)
    inv = 1.0 / (l * g + l2 * g2)
    f0, f1, g2 = f0 * g * inv, f1 * g * inv, g2 * inv
    c_mine.wait_recv()
    for i in range(q4):
        at = x * (2 * q4) + c * q4 + i
        mine_o[i] = o_ref[at] * column(f0, x, c, i) + mine_o[i] * column(f1, x, c, i)
    c_xo.wait_recv()
    for i in range(q4):
        att_send[i] = mine_o[i] + x_o[i] * column(g2, x, c, i)
    c_att = remote(att_send, att.at[pl.ds(c * q4, q4)], s_sem.at[5], r_sem.at[5], sib)
    c_att.start()
    for n in range(n_q):
        lhs[pl.ds(c * q4, q4), n * 128:(n + 1) * 128] = att_send[:, n, :].astype(jnp.bfloat16)
    c_att.wait_recv()
    for n in range(n_q):
        lhs[pl.ds((1 - c) * q4, q4), n * 128:(n + 1) * 128] = (
            att[pl.ds((1 - c) * q4, q4), n, :].astype(jnp.bfloat16))

    y_copy, x_copy, d_copy, e_copy = [], [], [], []
    for j in range(OUT_CHUNKS):
        w_copy(j).wait()
        part[j] = jnp.dot(lhs[...], w_buf[:, j * cc:(j + 1) * cc], preferred_element_type=jnp.float32)
        y_copy.append(remote(part.at[j], y_in.at[j], ys_sem.at[j], yr_sem.at[j], yn))
        y_copy[j].start()

    my_rows = pl.ds(pl.multiple_of(x * (2 * q4), 2 * q4), 2 * q4)
    xn_rows = pl.ds(pl.multiple_of((1 - x) * (2 * q4), 2 * q4), 2 * q4)

    def cols(start, j):
        return pl.ds(pl.multiple_of(start + j * cc, 128), cc)

    for j in range(OUT_CHUNKS):
        y_copy[j].wait_recv()
        fin[j] = h_ref[my_rows, cols(own_col, j)].astype(jnp.float32) + (part[j] + y_in[j])
        x_copy.append(remote(fin.at[j], x_in.at[j], xs_sem.at[j], xr_sem.at[j], xn))
        x_copy[j].start()
        d_copy.append(remote(fin.at[j], d_in.at[j], ds_sem.at[j], dr_sem.at[j], sib))
        d_copy[j].start()
        out_ref[my_rows, cols(own_col, j)] = fin[j].astype(jnp.bfloat16)
    for j in range(OUT_CHUNKS):
        x_copy[j].wait_recv()
        e_copy.append(remote(x_in.at[j], d_in2.at[j], es_sem.at[j], er_sem.at[j], sib))
        e_copy[j].start()
        out_ref[xn_rows, cols(own_col, j)] = x_in[j].astype(jnp.bfloat16)
        d_copy[j].wait_recv()
        out_ref[my_rows, cols(oth_col, j)] = d_in[j].astype(jnp.bfloat16)
    for j in range(OUT_CHUNKS):
        e_copy[j].wait_recv()
        out_ref[xn_rows, cols(oth_col, j)] = d_in2[j].astype(jnp.bfloat16)

    for cp in [c_ml, c_sib, c_mine, c_xml, c_xo, c_att] + y_copy + x_copy + d_copy + e_copy:
        cp.wait_send()


def solution(mesh):
    cache_spec = P('dp', 'sp', 'tp', None)

    def local_step(hidden, norm_scale, w_qkv, w_out, k_cache, v_cache, positions):
        n_seq, seq_local, kv_local, head = k_cache.shape
        d_model = hidden.shape[1]
        rows = seq_local * kv_local
        n_q = 4 * kv_local
        vm = pl.BlockSpec(memory_space=pltpu.VMEM)
        anyspace = pl.BlockSpec(memory_space=pltpu.HBM)
        smem = pl.BlockSpec(memory_space=pltpu.SMEM)
        f32, bf16 = jnp.float32, jnp.bfloat16
        k_upd, v_upd, o, ml = pl.pallas_call(
            attention_kernel,
            out_shape=(jax.ShapeDtypeStruct((n_seq, rows, head), bf16),
                       jax.ShapeDtypeStruct((n_seq, rows, head), bf16),
                       pltpu.VMEM((n_seq, n_q, head), f32),
                       pltpu.VMEM((2 * n_q, 128), f32)),
            in_specs=[smem, vm, vm, anyspace, anyspace, anyspace],
            out_specs=(anyspace, anyspace, vm, vm),
            scratch_shapes=[
                pltpu.VMEM((n_seq, rows, head), bf16),
                pltpu.VMEM((n_seq, rows, head), bf16),
                pltpu.VMEM((kv_local, d_model, 6 * head), bf16),
                pltpu.VMEM((n_seq, d_model), bf16),
                pltpu.VMEM((n_seq, n_q, head), f32),
                pltpu.VMEM((n_seq, 16, head), f32),
                pltpu.VMEM((n_seq, 16, head), f32),
                pltpu.VMEM((n_seq, head), f32),
                pltpu.VMEM((n_q, rows), jnp.int32),
                pltpu.SemaphoreType.DMA((kv_local, W_PARTS)),
                pltpu.SemaphoreType.DMA((CACHE_PARTS,)),
                pltpu.SemaphoreType.DMA((CACHE_PARTS,)),
                pltpu.SemaphoreType.DMA((CACHE_PARTS,)),
                pltpu.SemaphoreType.DMA((CACHE_PARTS,)),
            ],
            compiler_params=pltpu.CompilerParams(vmem_limit_bytes=52 * 1024 * 1024),
            name='attention',
        )(positions, hidden, norm_scale.reshape(d_model // 128, 128), w_qkv,
          k_cache.reshape(n_seq, rows, head), v_cache.reshape(n_seq, rows, head))

        q4 = n_seq // 4
        half_cols = d_model // 2
        cc = half_cols // OUT_CHUNKS
        dma = pltpu.SemaphoreType.DMA
        h_out = pl.pallas_call(
            finish_kernel,
            out_shape=jax.ShapeDtypeStruct((n_seq, d_model), bf16),
            in_specs=[vm, anyspace, vm, vm],
            out_specs=vm,
            scratch_shapes=[
                pltpu.VMEM((w_out.shape[0], half_cols), bf16),
                pltpu.VMEM((q4, n_q, head), f32),
                pltpu.VMEM((q4, n_q, head), f32),
                pltpu.VMEM((2 * n_q, 128), f32),
                pltpu.VMEM((q4, n_q, head), f32),
                pltpu.VMEM((2 * n_q, 128), f32),
                pltpu.VMEM((q4, n_q, head), f32),
                pltpu.VMEM((2 * n_q, 128), f32),
                pltpu.VMEM((2 * q4, n_q, head), f32),
                pltpu.VMEM((q4, n_q, head), f32),
                pltpu.VMEM((2 * q4, n_q * head), bf16),
                pltpu.VMEM((OUT_CHUNKS, 2 * q4, cc), f32),
                pltpu.VMEM((OUT_CHUNKS, 2 * q4, cc), f32),
                pltpu.VMEM((OUT_CHUNKS, 2 * q4, cc), f32),
                pltpu.VMEM((OUT_CHUNKS, 2 * q4, cc), f32),
                pltpu.VMEM((OUT_CHUNKS, 2 * q4, cc), f32),
                pltpu.VMEM((OUT_CHUNKS, 2 * q4, cc), f32),
                dma((OUT_CHUNKS,)), dma((6,)), dma((6,)),
                dma((OUT_CHUNKS,)), dma((OUT_CHUNKS,)),
                dma((OUT_CHUNKS,)), dma((OUT_CHUNKS,)),
                dma((OUT_CHUNKS,)), dma((OUT_CHUNKS,)),
                dma((OUT_CHUNKS,)), dma((OUT_CHUNKS,)),
            ],
            compiler_params=pltpu.CompilerParams(
                collective_id=0, has_side_effects=True, vmem_limit_bytes=56 * 1024 * 1024),
            name='finish',
        )(hidden, w_out, o, ml)
        return h_out, k_upd.reshape(k_cache.shape), v_upd.reshape(v_cache.shape)

    return jax.shard_map(
        local_step,
        mesh=mesh,
        in_specs=(P('dp', None), P(None), P(None, 'tp'), P('tp', None), cache_spec, cache_spec, P('dp')),
        out_specs=(P('dp', None), cache_spec, cache_spec),
        check_vma=False,
    )
```

time: 162 us -> 62.3 us (0.38)
  waiting for transfers between devices: 65.7 us -> 0 us
  Pallas kernels: 0 us -> 55.6 us
  matrix products: 33.2 us -> 0 us
  other arithmetic: 24.1 us -> 0 us
  blocking collectives: 15 us -> 0 us
  between operations: 14.2 us -> 0.67 us
  local copies, waits for them, and re-layouts: 8.72 us -> 5.64 us
    psum x2 -> x0, waiting for transfers between devices: 65.7 us -> none  [the longest x1 34.7 us: local_step(): proj_sum = lax.psum(head_part, 'tp')]
    pallas_call x0 -> x2, Pallas kernels: none -> 55.6 us  [the longest x1 28.9 us: local_step(): pl.pallas_call(attention_kernel, out_shape=(jax.ShapeDtypeStruct((n_seq,...]
    dot_general x4 -> x0, matrix products: 33.2 us -> none  [the longest x1 12.9 us: local_step(): jnp.dot(normed, w_qkv, preferred_element_type=jnp.float32)]
    pmax x1 -> x0, blocking collectives: 15 us -> none  [local_step(): global_max = lax.pmax(local_max, 'sp')]
    select_n x1 -> x0, other arithmetic: 13.8 us -> none  [local_step(): v_upd = jnp.where(new_row, grouped[:, :, q_per_kv + 1][:, None], v_cache)]
    convert_element_type x5 -> x0, other arithmetic: 4.33 us -> none  [the longest x1 2.11 us: local_step(): h_out = (hidden_f32 + proj_sum).astype(jnp.bfloat16)]
    reduce_sum x3 -> x0, other arithmetic: 3.31 us -> none  [the longest x1 1.35 us: layer_norm_bf16(): row_var = jnp.mean(centered * centered, axis=-1, keepdims=True)]
    unnamed x6 -> x11, local copies, waits for them, and re-layouts: 3.4 us -> 5.64 us
  transfers between devices with their start and end apart: 2 -> 0, of which waited for: 2 -> 0; matrix products, arithmetic and copies ran while one was open for 0% -> 0% of each run, Pallas kernels for 0% -> 0%
where the time goes in v1:
time: 62.3 us; the launch traced here: 61.9 us
  Pallas kernels  55.6 us (89%)
  local copies, waits for them, and re-layouts  5.64 us (9%)
  between operations  0.67 us (1%)
    pallas_call x1, Pallas kernels, local_step(): pl.pallas_call(attention_kernel, out_shape=(jax.ShapeDtypeStruct((n_seq,...  28.9 us
    pallas_call x1, Pallas kernels, local_step(): pl.pallas_call(finish_kernel, out_shape=jax.ShapeDtypeStruct((n_seq, d_mo...  26.7 us
    unnamed x11, local copies, waits for them, and re-layouts  5.64 us

profile of v1, /device:TPU:0, one launch (start us, length us, event | category | flops | bytes accessed | tf_op | source)
XLA Modules:
  0.0 61.9 jit_solution(3659233319733460253)
XLA Ops:
  0.6 0.0 copy-start
  0.6 1.0 %copy-done = bf16[64,4096]{1,0:T(8,128)(2,1)S(1)} copy-done((bf16[64,4096]{1,0:T(8,128)(2,1)S(1)}, bf16[64,4096]{1,0:T(8,128)(2,1)}, u32[]{:S(2)}) %copy-start) | copy-done | bytes 524312
  1.7 0.0 copy-start.3
  1.7 0.7 %copy-done.3 = bf16[4096]{0:T(1024)(128)(2,1)S(1)} copy-done((bf16[4096]{0:T(1024)(128)(2,1)S(1)}, bf16[4096]{0:T(1024)(128)(2,1)}, u32[]{:S(2)}) %copy-start.3) | copy-done | bytes 8216
  2.4 0.0 copy-start.4
  2.4 0.7 %copy-done.4 = s32[64]{0:T(128)S(1)} copy-done((s32[64]{0:T(128)S(1)}, s32[64]{0:T(128)}, u32[]{:S(2)}) %copy-start.4) | copy-done | bytes 280
  3.0 28.9 %attention.1 = (bf16[64,512,128]{2,1,0:T(8,128)(2,1)}, bf16[64,512,128]{2,1,0:T(8,128)(2,1)}, f32[64,16,128]{2,1,0:T(8,128)S(1)}, f32[32,128]{1,0:T(8,128)S(1)}) custom-call(s32[64]{0:T(128)S(1)} %copy-done.4, bf16[64,4096]{1,0:T(8,128)(2,1)S(1)} %copy-done, bf16[32,128]{1,0:T(8,128)(2,1)S(1)} %bitcast.5, bf16[4096,3072]{1,0:T(8,128)(2,1)} %w_ref.2, ...), custom_call_target="tpu_custom_call" | custom-call | tf_op jit(solution)/shard_map/attention/pallas_call | solution.py:303
  31.9 0.0 copy-start.1
  32.0 0.8 %copy-done.1 = f32[64,16,128]{2,1,0:T(8,128)} copy-done((f32[64,16,128]{2,1,0:T(8,128)}, f32[64,16,128]{2,1,0:T(8,128)S(1)}, u32[]{:S(2)}) %copy-start.1) | copy-done | bytes 524312
  32.7 0.0 copy-start.2
  32.7 0.6 copy-done.2
  33.3 26.7 %finish.1 = bf16[64,4096]{1,0:T(8,128)(2,1)} custom-call(bf16[64,4096]{1,0:T(8,128)(2,1)} %h_ref.3, bf16[2048,4096]{1,0:T(8,128)(2,1)} %w_ref.3, f32[64,16,128]{2,1,0:T(8,128)} %copy-done.1, f32[32,128]{1,0:T(8,128)} %copy-done.2), custom_call_target="tpu_custom_call" | custom-call | tf_op jit(solution)/shard_map/finish/pallas_call | solution.py:336
  60.1 1.9 %copy.11 = bf16[64,4096]{1,0:T(8,128)(2,1)} copy(bf16[64,4096]{1,0:T(8,128)(2,1)} %finish.1) | data formatting | bytes 1048576
Async XLA Ops:
  0.6 1.0 %copy-start = (bf16[64,4096]{1,0:T(8,128)(2,1)S(1)}, bf16[64,4096]{1,0:T(8,128)(2,1)}, u32[]{:S(2)}) copy-start(bf16[64,4096]{1,0:T(8,128)(2,1)} %h_ref.3) | copy-start | bytes 1572868
  1.7 0.7 %copy-start.3 = (bf16[4096]{0:T(1024)(128)(2,1)S(1)}, bf16[4096]{0:T(1024)(128)(2,1)}, u32[]{:S(2)}) copy-start(bf16[4096]{0:T(1024)(128)(2,1)} %param.8) | copy-start | bytes 24580
  2.4 0.7 %copy-start.4 = (s32[64]{0:T(128)S(1)}, s32[64]{0:T(128)}, u32[]{:S(2)}) copy-start(s32[64]{0:T(128)} %pos_ref.1) | copy-start | bytes 772
  31.9 0.8 %copy-start.1 = (f32[64,16,128]{2,1,0:T(8,128)}, f32[64,16,128]{2,1,0:T(8,128)S(1)}, u32[]{:S(2)}) copy-start(f32[64,16,128]{2,1,0:T(8,128)S(1)} %get-tuple-element.7.o_ref) | copy-start | bytes 1572868
  32.7 0.6 copy-start.2

commit v2 on v1

--- a/solution.py
+++ b/solution.py
@@ -10,17 +10,18 @@
 
 MESH = pl.DeviceIdType.MESH
 NEG = -1e30
-UNROLL = 4
+PV_LAG = 2
 W_PARTS = 2
 CACHE_PARTS = 8
 OUT_CHUNKS = 4
 LN_EPS = 1e-5
 
 
-def attention_kernel(pos_ref, h_ref, scale_ref, w_ref, kc_ref, vc_ref,
+def attention_kernel(pos_hbm, h_hbm, scale_hbm, w_ref, kc_ref, vc_ref,
                      ko_ref, vo_ref, o_ref, ml_ref,
-                     k_ref, v_ref, w_buf, u_ref, q_ref, kn_ref, vn_ref, ang_ref, idx_ref,
-                     w_sem, k_sem, v_sem, ko_sem, vo_sem):
+                     pos_ref, h_ref, scale_ref, k_ref, v_ref, w_buf, u_ref, q_ref, kn_ref, vn_ref,
+                     ang_ref, idx_ref, s_ref,
+                     in_sem, w_sem, k_sem, v_sem, ko_sem, vo_sem):
     n_seq, d_model = h_ref.shape
     rows = k_ref.shape[1]
     head = k_ref.shape[2]
@@ -31,6 +32,12 @@
     w_rows = d_model // W_PARTS
     c_rows = n_seq // CACHE_PARTS
 
+    small = [pltpu.make_async_copy(h_hbm, h_ref, in_sem.at[0]),
+             pltpu.make_async_copy(scale_hbm, scale_ref, in_sem.at[1]),
+             pltpu.make_async_copy(pos_hbm, pos_ref, in_sem.at[2])]
+    for cp in small:
+        cp.start()
+
     def w_copy(g, part):
         at = pl.ds(part * w_rows, w_rows)
         return pltpu.make_async_copy(
@@ -49,7 +56,32 @@
     for g in range(kv_local):
         for part in range(W_PARTS):
             w_copy(g, part).start()
-
+    for i in range(CACHE_PARTS):
+        for c in c_copies(i):
+            c.start(priority=1)
+
+    n_q = 4 * kv_local
+    col = lax.broadcasted_iota(jnp.int32, (n_q, rows), 1)
+    qg = lax.broadcasted_iota(jnp.int32, (n_q, rows), 0) // 4
+    idx_ref[...] = jnp.where(col % kv_local == qg, col // kv_local, 1 << 20)
+
+    lane = lax.broadcasted_iota(jnp.int32, (1, head), 1)
+    half = head // 2
+    inv_freq = jnp.exp((lane % half).astype(jnp.float32) * (-2.0 * math.log(500000.0) / head))
+    small[2].wait()
+
+    def fill(b, _):
+        ang_ref[pl.ds(b, 1), :] = jnp.full((1, head), pos_ref[b].astype(jnp.float32)) * inv_freq
+        return 0
+    lax.fori_loop(0, n_seq, fill, 0)
+    cos = jnp.cos(ang_ref[...])
+    sin = jnp.sin(ang_ref[...]) * jnp.where(lane < half, -1.0, 1.0)
+
+    def rope(x):
+        return (x * cos + pltpu.roll(x, half, 1) * sin).astype(jnp.bfloat16).astype(jnp.float32)
+
+    small[0].wait()
+    small[1].wait()
     blocks = d_model // 128
     total = jnp.zeros((n_seq, 128), jnp.float32)
     for i in range(blocks):
@@ -66,34 +98,10 @@
         u_ref[:, i * 128:(i + 1) * 128] = (
             cen * rstd * scale_ref[i:i + 1, :].astype(jnp.float32)).astype(jnp.bfloat16)
 
-    lane = lax.broadcasted_iota(jnp.int32, (1, head), 1)
-    half = head // 2
-    inv_freq = jnp.exp((lane % half).astype(jnp.float32) * (-2.0 * math.log(500000.0) / head))
-
-    def fill(b, _):
-        ang_ref[pl.ds(b, 1), :] = jnp.full((1, head), pos_ref[b].astype(jnp.float32)) * inv_freq
-        return 0
-    lax.fori_loop(0, n_seq, fill, 0)
-    cos = jnp.cos(ang_ref[...])
-    sin = jnp.sin(ang_ref[...]) * jnp.where(lane < half, -1.0, 1.0)
-
-    def rope(x):
-        return (x * cos + pltpu.roll(x, half, 1) * sin).astype(jnp.bfloat16).astype(jnp.float32)
-
-    n_q = 4 * kv_local
-    col = lax.broadcasted_iota(jnp.int32, (n_q, rows), 1)
-    qg = lax.broadcasted_iota(jnp.int32, (n_q, rows), 0) // 4
-    idx_ref[...] = jnp.where(col % kv_local == qg, col // kv_local, 1 << 20)
-
-    started = 0
     for g in range(kv_local):
         acc = jnp.zeros((n_seq, group_cols), jnp.float32)
         for part in range(W_PARTS):
             w_copy(g, part).wait()
-            if started < CACHE_PARTS:
-                for c in c_copies(started):
-                    c.start()
-                started += 1
             at = pl.ds(part * w_rows, w_rows)
             acc += jnp.dot(u_ref[:, at], w_buf[g, at, :], preferred_element_type=jnp.float32)
         qkv = jnp.clip(acc.astype(jnp.bfloat16).astype(jnp.float32), -8.0, 8.0)
@@ -104,52 +112,59 @@
         for r in range(16 // kv_local):
             kn_ref[:, r * kv_local + g, :] = kn
             vn_ref[:, r * kv_local + g, :] = vn
-    for i in range(started, CACHE_PARTS):
-        for c in c_copies(i):
-            c.start()
 
     scale = head ** -0.5
     per = 16 // kv_local
     row16 = lax.broadcasted_iota(jnp.int32, (16, head), 0) // kv_local
     lane_id = lax.broadcasted_iota(jnp.int32, (n_q, 128), 1)
+    last = rows // 16 - 1
 
     def insert(b):
         p = pos_ref[b] - base
-
-        @pl.when((p >= 0) & (p < rows // kv_local))
-        def _():
-            at = pl.ds(pl.multiple_of((p // per) * 16, 16), 16)
-            hit = row16 == p % per
-            k_ref[b, at, :] = jnp.where(hit, kn_ref[b], k_ref[b, at, :].astype(jnp.float32)).astype(jnp.bfloat16)
-            v_ref[b, at, :] = jnp.where(hit, vn_ref[b], v_ref[b, at, :].astype(jnp.float32)).astype(jnp.bfloat16)
-
-    def attend(b, m_all, l_all):
-        p = pos_ref[b] - base
-        s = lax.dot_general(q_ref[b].astype(jnp.bfloat16), k_ref[b], (((1,), (1,)), ((), ())),
-                            preferred_element_type=jnp.float32)
-        s = jnp.where(idx_ref[...] <= p, s * scale, NEG)
-        m = jnp.max(s, axis=1, keepdims=True)
-        e = jnp.exp(s - m)
-        l = jnp.sum(e, axis=1, keepdims=True)
-        o_ref[b] = jnp.dot(e.astype(jnp.bfloat16), v_ref[b], preferred_element_type=jnp.float32)
-        return jnp.where(lane_id == b, m, m_all), jnp.where(lane_id == b, l, l_all)
+        tile = jnp.clip(p // per, 0, last)
+        at = pl.ds(pl.multiple_of(tile * 16, 16), 16)
+        hit = row16 == p - tile * per
+        k_ref[b, at, :] = jnp.where(hit, kn_ref[b], k_ref[b, at, :].astype(jnp.float32)).astype(jnp.bfloat16)
+        v_ref[b, at, :] = jnp.where(hit, vn_ref[b], v_ref[b, at, :].astype(jnp.float32)).astype(jnp.bfloat16)
+
+    def scores(b, slot, k):
+        s_ref[slot, k] = lax.dot_general(
+            q_ref[b].astype(jnp.bfloat16), k_ref[b], (((1,), (1,)), ((), ())),
+            preferred_element_type=jnp.float32)
+
+    def arrive(i):
+        for c in c_copies(i):
+            c.wait()
+        for k in range(c_rows):
+            insert(i * c_rows + k)
+        for c in out_copies(i):
+            c.start(priority=1)
 
     m_all = jnp.zeros((n_q, 128), jnp.float32)
     l_all = jnp.zeros((n_q, 128), jnp.float32)
+    arrive(0)
+    for k in range(c_rows):
+        scores(k, 0, k)
     for i in range(CACHE_PARTS):
-        for c in c_copies(i):
-            c.wait()
-
-        def step(t, carry):
-            b0 = i * c_rows + t * UNROLL
-            for k in range(UNROLL):
-                insert(b0 + k)
-            for k in range(UNROLL):
-                carry = attend(b0 + k, *carry)
-            return carry
-        m_all, l_all = lax.fori_loop(0, c_rows // UNROLL, step, (m_all, l_all))
-        for c in out_copies(i):
-            c.start()
+        more = i + 1 < CACHE_PARTS
+        if more:
+            arrive(i + 1)
+        weights = [None] * c_rows
+        for k in range(c_rows + PV_LAG):
+            if k < c_rows:
+                b = i * c_rows + k
+                if more:
+                    scores(b + c_rows, (i + 1) % 2, k)
+                s = jnp.where(idx_ref[...] <= pos_ref[b] - base, s_ref[i % 2, k] * scale, NEG)
+                m = jnp.max(s, axis=1, keepdims=True)
+                e = jnp.exp(s - m)
+                l = jnp.sum(e, axis=1, keepdims=True)
+                weights[k] = e.astype(jnp.bfloat16)
+                m_all = jnp.where(lane_id == b, m, m_all)
+                l_all = jnp.where(lane_id == b, l, l_all)
+            if k >= PV_LAG:
+                b = i * c_rows + k - PV_LAG
+                o_ref[b] = jnp.dot(weights[k - PV_LAG], v_ref[b], preferred_element_type=jnp.float32)
     ml_ref[0:n_q, :] = m_all
     ml_ref[n_q:, :] = l_all
     for i in range(CACHE_PARTS):
@@ -298,7 +313,6 @@
         n_q = 4 * kv_local
         vm = pl.BlockSpec(memory_space=pltpu.VMEM)
         anyspace = pl.BlockSpec(memory_space=pltpu.HBM)
-        smem = pl.BlockSpec(memory_space=pltpu.SMEM)
         f32, bf16 = jnp.float32, jnp.bfloat16
         k_upd, v_upd, o, ml = pl.pallas_call(
             attention_kernel,
@@ -306,9 +320,12 @@
                        jax.ShapeDtypeStruct((n_seq, rows, head), bf16),
                        pltpu.VMEM((n_seq, n_q, head), f32),
                        pltpu.VMEM((2 * n_q, 128), f32)),
-            in_specs=[smem, vm, vm, anyspace, anyspace, anyspace],
+            in_specs=[anyspace] * 6,
             out_specs=(anyspace, anyspace, vm, vm),
             scratch_shapes=[
+                pltpu.SMEM((n_seq,), jnp.int32),
+                pltpu.VMEM((n_seq, d_model), bf16),
+                pltpu.VMEM((d_model // 128, 128), bf16),
                 pltpu.VMEM((n_seq, rows, head), bf16),
                 pltpu.VMEM((n_seq, rows, head), bf16),
                 pltpu.VMEM((kv_local, d_model, 6 * head), bf16),
@@ -318,13 +335,15 @@
                 pltpu.VMEM((n_seq, 16, head), f32),
                 pltpu.VMEM((n_seq, head), f32),
                 pltpu.VMEM((n_q, rows), jnp.int32),
+                pltpu.VMEM((2, n_seq // CACHE_PARTS, n_q, rows), f32),
+                pltpu.SemaphoreType.DMA((3,)),
                 pltpu.SemaphoreType.DMA((kv_local, W_PARTS)),
                 pltpu.SemaphoreType.DMA((CACHE_PARTS,)),
                 pltpu.SemaphoreType.DMA((CACHE_PARTS,)),
                 pltpu.SemaphoreType.DMA((CACHE_PARTS,)),
                 pltpu.SemaphoreType.DMA((CACHE_PARTS,)),
             ],
-            compiler_params=pltpu.CompilerParams(vmem_limit_bytes=52 * 1024 * 1024),
+            compiler_params=pltpu.CompilerParams(vmem_limit_bytes=54 * 1024 * 1024),
             name='attention',
         )(positions, hidden, norm_scale.reshape(d_model // 128, 128), w_qkv,
           k_cache.reshape(n_seq, rows, head), v_cache.reshape(n_seq, rows, head))
@@ -363,7 +382,7 @@
                 dma((OUT_CHUNKS,)), dma((OUT_CHUNKS,)),
             ],
             compiler_params=pltpu.CompilerParams(
-                collective_id=0, has_side_effects=True, vmem_limit_bytes=56 * 1024 * 1024),
+                collective_id=0, has_side_effects=True, vmem_limit_bytes=52 * 1024 * 1024),
             name='finish',
         )(hidden, w_out, o, ml)
         return h_out, k_upd.reshape(k_cache.shape), v_upd.reshape(v_cache.shape)

time: 62.3 us -> 46.5 us (0.75)
  Pallas kernels: 55.6 us -> 45 us
  local copies, waits for them, and re-layouts: 5.64 us -> 0.8 us
    pallas_call x1, Pallas kernels: 28.9 us -> 20.5 us  [local_step(): pl.pallas_call(attention_kernel, out_shape=(jax.ShapeDtypeStruct((n_seq,...]
    unnamed x11 -> x3, local copies, waits for them, and re-layouts: 5.64 us -> 0.8 us
    pallas_call x1, Pallas kernels: 26.7 us -> 24.5 us  [local_step(): pl.pallas_call(finish_kernel, out_shape=jax.ShapeDtypeStruct((n_seq, d_mo...]
where the time goes in v2:
time: 46.5 us; the launch traced here: 46.4 us
  Pallas kernels  45 us (97%)
  local copies, waits for them, and re-layouts  0.8 us (2%)
  between operations  0.66 us (1%)
    pallas_call x1, Pallas kernels, local_step(): pl.pallas_call(finish_kernel, out_shape=jax.ShapeDtypeStruct((n_seq, d_mo...  24.5 us
    pallas_call x1, Pallas kernels, local_step(): pl.pallas_call(attention_kernel, out_shape=(jax.ShapeDtypeStruct((n_seq,...  20.5 us

profile of v2, /device:TPU:0, one launch (start us, length us, event | category | flops | bytes accessed | tf_op | source)
XLA Modules:
  0.0 46.4 jit_solution(18178472108156163881)
XLA Ops:
  0.6 0.0 copy-start
  0.6 20.5 %attention.1 = (bf16[64,512,128]{2,1,0:T(8,128)(2,1)}, bf16[64,512,128]{2,1,0:T(8,128)(2,1)}, f32[64,16,128]{2,1,0:T(8,128)S(1)}, f32[32,128]{1,0:T(8,128)S(1)}) custom-call(s32[64]{0:T(128)} %pos_hbm.1, bf16[64,4096]{1,0:T(8,128)(2,1)} %h_ref.1, bf16[32,128]{1,0:T(8,128)(2,1)} %bitcast.7, bf16[4096,3072]{1,0:T(8,128)(2,1)} %w_ref.2, ...), custom_call_target="tpu_custom_call" | custom-call | tf_op jit(solution)/shard_map/attention/pallas_call | solution.py:317
  21.1 0.0 copy-done
  21.1 24.5 %finish.1 = bf16[64,4096]{1,0:T(8,128)(2,1)S(1)} custom-call(bf16[64,4096]{1,0:T(8,128)(2,1)S(1)} %copy-done, bf16[2048,4096]{1,0:T(8,128)(2,1)} %w_ref.3, f32[64,16,128]{2,1,0:T(8,128)S(1)} %get-tuple-element.7.o_ref, f32[32,128]{1,0:T(8,128)S(1)} %get-tuple-element.8.ml_ref), custom_call_target="tpu_custom_call" | custom-call | tf_op jit(solution)/shard_map/finish/pallas_call | solution.py:355
  45.6 0.8 %copy.11 = bf16[64,4096]{1,0:T(8,128)(2,1)} copy(bf16[64,4096]{1,0:T(8,128)(2,1)S(1)} %finish.1) | data formatting | bytes 1048576
Async XLA Ops:
  0.6 20.5 %copy-start = (bf16[64,4096]{1,0:T(8,128)(2,1)S(1)}, bf16[64,4096]{1,0:T(8,128)(2,1)}, u32[]{:S(2)}) copy-start(bf16[64,4096]{1,0:T(8,128)(2,1)} %h_ref.1) | copy-start | bytes 1572868

commit v3 on v0

v3 whole, which is shorter than its diff:
```python
import math

import jax
import jax.numpy as jnp
from jax import lax
from jax.experimental import pallas as pl
from jax.experimental.pallas import tpu as pltpu
from jax.sharding import PartitionSpec as P

MESH = pl.DeviceIdType.MESH
NEG = -1e30
PV_LAG = 4
W_HEADS = 6
PART = 8
OUT_CHUNKS = 8
LN_EPS = 1e-5


def quarters(n_seq):
    sp = lax.axis_index('sp')
    x, c = sp // 2, sp % 2
    q = n_seq // 4

    def start(xx, cc):
        return pl.multiple_of((xx * 2 + cc) * q, q)
    return [start(1 - x, c), start(1 - x, 1 - c), start(x, 1 - c), start(x, c)]


def insert_row(k_ref, v_ref, at_b, p, kn, vn):
    rows, head = k_ref.shape[1:]
    kv_local = rows // 128
    per = 16 // kv_local
    tile = jnp.clip(p // per, 0, rows // 16 - 1)
    at = pl.ds(pl.multiple_of(tile * 16, 16), 16)
    hit = lax.broadcasted_iota(jnp.int32, (16, head), 0) // kv_local == p - tile * per
    k_ref[at_b, at, :] = jnp.where(hit, kn, k_ref[at_b, at, :].astype(jnp.float32)).astype(jnp.bfloat16)
    v_ref[at_b, at, :] = jnp.where(hit, vn, v_ref[at_b, at, :].astype(jnp.float32)).astype(jnp.bfloat16)


def row_index(n_q, rows):
    kv_local = n_q // 4
    col = lax.broadcasted_iota(jnp.int32, (n_q, rows), 1)
    qg = lax.broadcasted_iota(jnp.int32, (n_q, rows), 0) // 4
    return jnp.where(col % kv_local == qg, col // kv_local, 1 << 20)


def attend_parts(parts, arrive, q_at, p_at, k_ref, v_ref, idx_ref, s_ref, out_at):
    scale = k_ref.shape[2] ** -0.5

    def scores(b, slot, k):
        s_ref[slot, k] = lax.dot_general(
            q_at(b).astype(jnp.bfloat16), k_ref[b], (((1,), (1,)), ((), ())),
            preferred_element_type=jnp.float32)

    arrive(0)
    for k, b in enumerate(parts[0]):
        scores(b, 0, k)
    for i, part in enumerate(parts):
        more = i + 1 < len(parts)
        if more:
            arrive(i + 1)
        held = [None] * len(part)
        for k in range(len(part) + PV_LAG):
            if k < len(part):
                if more:
                    scores(parts[i + 1][k], (i + 1) % 2, k)
                s = jnp.where(idx_ref[...] <= p_at(part[k]), s_ref[i % 2, k] * scale, NEG)
                m = jnp.max(s, axis=1, keepdims=True)
                e = jnp.exp(s - m)
                held[k] = (e.astype(jnp.bfloat16), m, jnp.sum(e, axis=1, keepdims=True))
            if k >= PV_LAG:
                b = part[k - PV_LAG]
                e, m, l = held[k - PV_LAG]
                out_at(b, jnp.dot(e, v_ref[b], preferred_element_type=jnp.float32), m, l)


def put_stats(tile, lane_id, k, m, l):
    return jnp.where(lane_id == k, m, jnp.where(lane_id == 64 + k, l, tile))


def first_kernel(pos_hbm, h_hbm, scale_hbm, w_ref, kc_ref, vc_ref,
                 k_ref, v_ref, pay0, pay1, pay2, q_own, kn_own, vn_own,
                 pos_ref, h_ref, scale_ref, w_buf, u_ref, q_ref, kn_ref, vn_ref,
                 ang_ref, idx_ref, s_ref,
                 in_sem, w_sem, k_sem, v_sem):
    n_seq, d_model = h_ref.shape
    rows = k_ref.shape[1]
    head = k_ref.shape[2]
    kv_local = w_ref.shape[1] // (6 * head)
    n_q = 4 * kv_local
    base = lax.axis_index('sp') * (rows // kv_local)
    starts = quarters(n_seq)
    q4 = n_seq // 4
    per_slot = q4 // PART

    w_chunks, _, w_cols = w_buf.shape

    small = [pltpu.make_async_copy(h_hbm, h_ref, in_sem.at[0]),
             pltpu.make_async_copy(scale_hbm, scale_ref, in_sem.at[1]),
             pltpu.make_async_copy(pos_hbm, pos_ref, in_sem.at[2])]
    for cp in small:
        cp.start()

    def w_copy(t):
        return pltpu.make_async_copy(w_ref.at[:, pl.ds(t * w_cols, w_cols)], w_buf.at[t], w_sem.at[t])

    def c_copies(i):
        src = pl.ds(starts[i // per_slot] + (i % per_slot) * PART, PART)
        dst = pl.ds(i * PART, PART)
        return (pltpu.make_async_copy(kc_ref.at[src], k_ref.at[dst], k_sem.at[i]),
                pltpu.make_async_copy(vc_ref.at[src], v_ref.at[dst], v_sem.at[i]))

    for t in range(w_chunks):
        w_copy(t).start()
    for i in range(3 * per_slot):
        for c in c_copies(i):
            c.start(priority=1)

    idx_ref[...] = row_index(n_q, rows)

    lane = lax.broadcasted_iota(jnp.int32, (1, head), 1)
    half = head // 2
    inv_freq = jnp.exp((lane % half).astype(jnp.float32) * (-2.0 * math.log(500000.0) / head))
    small[2].wait()

    def fill(b, _):
        ang_ref[pl.ds(b, 1), :] = jnp.full((1, head), pos_ref[b].astype(jnp.float32)) * inv_freq
        return 0
    lax.fori_loop(0, n_seq, fill, 0)
    cos = jnp.cos(ang_ref[...])
    sin = jnp.sin(ang_ref[...]) * jnp.where(lane < half, -1.0, 1.0)

    def rope(x):
        return (x * cos + pltpu.roll(x, half, 1) * sin).astype(jnp.bfloat16).astype(jnp.float32)

    small[0].wait()
    small[1].wait()
    blocks = d_model // 128
    total = jnp.zeros((n_seq, 128), jnp.float32)
    for i in range(blocks):
        total += h_ref[:, i * 128:(i + 1) * 128].astype(jnp.float32)
    mean = jnp.sum(total, axis=1, keepdims=True) * (1.0 / d_model)
    total = jnp.zeros((n_seq, 128), jnp.float32)
    for i in range(blocks):
        cen = h_ref[:, i * 128:(i + 1) * 128].astype(jnp.float32) - mean
        total += cen * cen
    var = jnp.sum(total, axis=1, keepdims=True) * (1.0 / d_model)
    rstd = lax.rsqrt(var + LN_EPS)
    for i in range(blocks):
        cen = h_ref[:, i * 128:(i + 1) * 128].astype(jnp.float32) - mean
        u_ref[:, i * 128:(i + 1) * 128] = (
            cen * rstd * scale_ref[i:i + 1, :].astype(jnp.float32)).astype(jnp.bfloat16)

    for t in range(w_chunks):
        w_copy(t).wait()
        acc = jnp.dot(u_ref[...], w_buf[t], preferred_element_type=jnp.float32)
        qkv = jnp.clip(acc.astype(jnp.bfloat16).astype(jnp.float32), -8.0, 8.0)
        for j in range(W_HEADS):
            g, kind = divmod(t * W_HEADS + j, 6)
            val = qkv[:, j * head:(j + 1) * head]
            if kind < 4:
                q_ref[:, g * 4 + kind, :] = rope(val)
                continue
            new_ref, new = (kn_ref, rope(val)) if kind == 4 else (vn_ref, val)
            for r in range(16 // kv_local):
                new_ref[:, r * kv_local + g, :] = new

    pays = [pay0, pay1, pay2]
    lane_id = lax.broadcasted_iota(jnp.int32, (n_q, 128), 1)
    stats = [jnp.zeros((n_q, 128), jnp.float32) for _ in pays]

    def seq(b):
        return starts[b // q4] + b % q4

    def arrive(i):
        for c in c_copies(i):
            c.wait()
        for k in range(PART):
            b = i * PART + k
            insert_row(k_ref, v_ref, b, pos_ref[seq(b)] - base, kn_ref[seq(b)], vn_ref[seq(b)])

    def out_at(b, o, m, l):
        pays[b // q4][b % q4] = o
        stats[b // q4] = put_stats(stats[b // q4], lane_id, b % q4, m, l)

    parts = [list(range(i * PART, (i + 1) * PART)) for i in range(3 * per_slot)]
    attend_parts(parts, arrive, lambda b: q_ref[seq(b)], lambda b: pos_ref[seq(b)] - base,
                 k_ref, v_ref, idx_ref, s_ref, out_at)
    for pay, tile in zip(pays, stats):
        pay[q4] = tile
    own = pl.ds(starts[3], q4)
    q_own[...] = q_ref[own]
    kn_own[...] = kn_ref[own]
    vn_own[...] = vn_ref[own]


def second_kernel(pos_hbm, q_ref, kn_ref, vn_ref, k3_ref, v3_ref, kc_ref, vc_ref,
                  ko_ref, vo_ref, pay_ref,
                  pos_ref, k_ref, v_ref, idx_ref, s_ref,
                  in_sem, k_sem, v_sem, o_sem, o3_sem):
    n_seq = ko_ref.shape[0]
    rows = k_ref.shape[1]
    n_q = q_ref.shape[1]
    base = lax.axis_index('sp') * (rows // (n_q // 4))
    starts = quarters(n_seq)
    q4 = n_seq // 4
    per_slot = q4 // PART

    pos_copy = pltpu.make_async_copy(pos_hbm, pos_ref, in_sem.at[0])
    pos_copy.start()

    def c_copies(i):
        src = pl.ds(starts[3] + i * PART, PART)
        dst = pl.ds(i * PART, PART)
        return (pltpu.make_async_copy(kc_ref.at[src], k_ref.at[dst], k_sem.at[i]),
                pltpu.make_async_copy(vc_ref.at[src], v_ref.at[dst], v_sem.at[i]))

    def o_copies(i):
        dst = pl.ds(starts[3] + i * PART, PART)
        src = pl.ds(i * PART, PART)
        return (pltpu.make_async_copy(k_ref.at[src], ko_ref.at[dst], o_sem.at[0, i]),
                pltpu.make_async_copy(v_ref.at[src], vo_ref.at[dst], o_sem.at[1, i]))

    def o3_copies(i):
        dst = pl.ds(starts[i], q4)
        src = pl.ds(i * q4, q4)
        return (pltpu.make_async_copy(k3_ref.at[src], ko_ref.at[dst], o3_sem.at[0, i]),
                pltpu.make_async_copy(v3_ref.at[src], vo_ref.at[dst], o3_sem.at[1, i]))

    for i in range(per_slot):
        for c in c_copies(i):
            c.start()
    for i in range(3):
        for c in o3_copies(i):
            c.start(priority=1)
    idx_ref[...] = row_index(n_q, rows)
    pos_copy.wait()

    lane_id = lax.broadcasted_iota(jnp.int32, (n_q, 128), 1)
    stats = [jnp.zeros((n_q, 128), jnp.float32)]

    def arrive(i):
        for c in c_copies(i):
            c.wait()
        for k in range(PART):
            b = i * PART + k
            insert_row(k_ref, v_ref, b, pos_ref[starts[3] + b] - base, kn_ref[b], vn_ref[b])
        for c in o_copies(i):
            c.start(priority=1)

    def out_at(b, o, m, l):
        pay_ref[b] = o
        stats[0] = put_stats(stats[0], lane_id, b, m, l)

    parts = [list(range(i * PART, (i + 1) * PART)) for i in range(per_slot)]
    attend_parts(parts, arrive, lambda b: q_ref[b], lambda b: pos_ref[starts[3] + b] - base,
                 k_ref, v_ref, idx_ref, s_ref, out_at)
    pay_ref[q4] = stats[0]
    for i in range(3):
        for c in o3_copies(i):
            c.wait()
    for i in range(per_slot):
        for c in o_copies(i):
            c.wait()


def finish_kernel(h_ref, w_ref, p0_ref, p1_ref, p2_ref, p3_ref, out_ref,
                  w_buf, att, att_send, lhs, part, y_in, fin, x_in, d_in, d_in2,
                  w_sem, a_sem, ys_sem, yr_sem, xs_sem, xr_sem, ds_sem, dr_sem, es_sem, er_sem):
    n_q = p0_ref.shape[1]
    sp = lax.axis_index('sp')
    tp = lax.axis_index('tp')
    x, c = sp // 2, sp % 2
    sib = {'sp': x * 2 + (1 - c)}
    xn = {'sp': (1 - x) * 2 + c}
    yn = {'tp': 1 - tp}

    half_cols = w_buf.shape[1]
    cc = half_cols // OUT_CHUNKS
    q4 = att_send.shape[0]
    own_col = c * half_cols
    oth_col = (1 - c) * half_cols

    def w_copy(j):
        return pltpu.make_async_copy(
            w_ref.at[:, pl.ds(pl.multiple_of(own_col + j * cc, 128), cc)],
            w_buf.at[:, pl.ds(j * cc, cc)], w_sem.at[j])

    for j in range(OUT_CHUNKS):
        w_copy(j).start()

    barrier = pltpu.get_barrier_semaphore()
    for dev in (sib, xn, yn):
        pl.semaphore_signal(barrier, inc=1, device_id=dev, device_id_type=MESH)

    def remote(src, dst, ssem, rsem, dev):
        return pltpu.make_async_remote_copy(src_ref=src, dst_ref=dst, send_sem=ssem, recv_sem=rsem,
                                            device_id=dev, device_id_type=MESH)

    pays = [p0_ref, p1_ref, p2_ref, p3_ref]
    maxes = [p[q4] for p in pays]
    sums = [pltpu.roll(m, 64, 1) for m in maxes]
    top = jnp.maximum(jnp.maximum(maxes[0], maxes[1]), jnp.maximum(maxes[2], maxes[3]))
    factors = [jnp.exp(m - top) for m in maxes]
    inv = 1.0 / sum(l * f for l, f in zip(sums, factors))
    factors = [f * inv for f in factors]
    for i in range(q4):
        att_send[i] = sum(p[i] * jnp.broadcast_to(f[:, i:i + 1], (n_q, 128)) for p, f in zip(pays, factors))

    pl.semaphore_wait(barrier, 3)
    c_att = remote(att_send, att, a_sem.at[0], a_sem.at[1], sib)
    c_att.start()
    for n in range(n_q):
        lhs[pl.ds(c * q4, q4), n * 128:(n + 1) * 128] = att_send[:, n, :].astype(jnp.bfloat16)
    c_att.wait_recv()
    for n in range(n_q):
        lhs[pl.ds((1 - c) * q4, q4), n * 128:(n + 1) * 128] = att[:, n, :].astype(jnp.bfloat16)

    y_copy, x_copy, d_copy, e_copy = [], [], [], []
    for j in range(OUT_CHUNKS):
        w_copy(j).wait()
        part[j] = jnp.dot(lhs[...], w_buf[:, j * cc:(j + 1) * cc], preferred_element_type=jnp.float32)
        y_copy.append(remote(part.at[j], y_in.at[j], ys_sem.at[j], yr_sem.at[j], yn))
        y_copy[j].start()

    my_rows = pl.ds(pl.multiple_of(x * (2 * q4), 2 * q4), 2 * q4)
    xn_rows = pl.ds(pl.multiple_of((1 - x) * (2 * q4), 2 * q4), 2 * q4)

    def cols(start, j):
        return pl.ds(pl.multiple_of(start + j * cc, 128), cc)

    for j in range(OUT_CHUNKS):
        y_copy[j].wait_recv()
        fin[j] = h_ref[my_rows, cols(own_col, j)].astype(jnp.float32) + (part[j] + y_in[j])
        x_copy.append(remote(fin.at[j], x_in.at[j], xs_sem.at[j], xr_sem.at[j], xn))
        x_copy[j].start()
        d_copy.append(remote(fin.at[j], d_in.at[j], ds_sem.at[j], dr_sem.at[j], sib))
        d_copy[j].start()
        out_ref[my_rows, cols(own_col, j)] = fin[j].astype(jnp.bfloat16)
    for j in range(OUT_CHUNKS):
        x_copy[j].wait_recv()
        e_copy.append(remote(x_in.at[j], d_in2.at[j], es_sem.at[j], er_sem.at[j], sib))
        e_copy[j].start()
        out_ref[xn_rows, cols(own_col, j)] = x_in[j].astype(jnp.bfloat16)
        d_copy[j].wait_recv()
        out_ref[my_rows, cols(oth_col, j)] = d_in[j].astype(jnp.bfloat16)
    for j in range(OUT_CHUNKS):
        e_copy[j].wait_recv()
        out_ref[xn_rows, cols(oth_col, j)] = d_in2[j].astype(jnp.bfloat16)

    for cp in [c_att] + y_copy + x_copy + d_copy + e_copy:
        cp.wait_send()


def solution(mesh):
    cache_spec = P('dp', 'sp', 'tp', None)

    def local_step(hidden, norm_scale, w_qkv, w_out, k_cache, v_cache, positions):
        n_seq, seq_local, kv_local, head = k_cache.shape
        d_model = hidden.shape[1]
        rows = seq_local * kv_local
        n_q = 4 * kv_local
        q4 = n_seq // 4
        vm = pl.BlockSpec(memory_space=pltpu.VMEM)
        hbm = pl.BlockSpec(memory_space=pltpu.HBM)
        dma = pltpu.SemaphoreType.DMA
        f32, bf16 = jnp.float32, jnp.bfloat16
        payload = pltpu.VMEM((q4 + 1, n_q, head), f32)
        k_rows = k_cache.reshape(n_seq, rows, head)
        v_rows = v_cache.reshape(n_seq, rows, head)
        slots = 3 * q4 // PART

        def pin(a):
            return pltpu.with_memory_space_constraint(a, pltpu.HBM)

        k3, v3, pay0, pay1, pay2, q_own, kn_own, vn_own = pl.pallas_call(
            first_kernel,
            out_shape=(pltpu.VMEM((3 * q4, rows, head), bf16), pltpu.VMEM((3 * q4, rows, head), bf16),
                       payload, payload, payload,
                       pltpu.VMEM((q4, n_q, head), f32), pltpu.VMEM((q4, 16, head), f32),
                       pltpu.VMEM((q4, 16, head), f32)),
            in_specs=[hbm] * 6,
            out_specs=(vm,) * 8,
            scratch_shapes=[
                pltpu.SMEM((n_seq,), jnp.int32),
                pltpu.VMEM((n_seq, d_model), bf16),
                pltpu.VMEM((d_model // 128, 128), bf16),
                pltpu.VMEM((6 * kv_local // W_HEADS, d_model, W_HEADS * head), bf16),
                pltpu.VMEM((n_seq, d_model), bf16),
                pltpu.VMEM((n_seq, n_q, head), f32),
                pltpu.VMEM((n_seq, 16, head), f32),
                pltpu.VMEM((n_seq, 16, head), f32),
                pltpu.VMEM((n_seq, head), f32),
                pltpu.VMEM((n_q, rows), jnp.int32),
                pltpu.VMEM((2, PART, n_q, rows), f32),
                dma((3,)), dma((6 * kv_local // W_HEADS,)), dma((slots,)), dma((slots,)),
            ],
            compiler_params=pltpu.CompilerParams(vmem_limit_bytes=40 * 1024 * 1024),
            cost_estimate=pl.CostEstimate(flops=2 * 10**10, bytes_accessed=4 * 10**7, transcendentals=0),
            name='first',
        )(*map(pin, (positions, hidden, norm_scale.reshape(d_model // 128, 128), w_qkv, k_rows, v_rows)))

        got0 = lax.ppermute(pay0, 'sp', [(i, i ^ 2) for i in range(4)])
        got1 = lax.ppermute(pay1, 'sp', [(i, 3 - i) for i in range(4)])
        got2 = lax.ppermute(pay2, 'sp', [(i, i ^ 1) for i in range(4)])

        k_upd, v_upd, mine = pl.pallas_call(
            second_kernel,
            out_shape=(jax.ShapeDtypeStruct((n_seq, rows, head), bf16),
                       jax.ShapeDtypeStruct((n_seq, rows, head), bf16), payload),
            in_specs=[hbm, vm, vm, vm, vm, vm, hbm, hbm],
            out_specs=(hbm, hbm, vm),
            scratch_shapes=[
                pltpu.SMEM((n_seq,), jnp.int32),
                pltpu.VMEM((q4, rows, head), bf16),
                pltpu.VMEM((q4, rows, head), bf16),
                pltpu.VMEM((n_q, rows), jnp.int32),
                pltpu.VMEM((2, PART, n_q, rows), f32),
                dma((1,)), dma((q4 // PART,)), dma((q4 // PART,)), dma((2, q4 // PART)), dma((2, 3)),
            ],
            compiler_params=pltpu.CompilerParams(vmem_limit_bytes=40 * 1024 * 1024),
            cost_estimate=pl.CostEstimate(flops=2 * 10**10, bytes_accessed=4 * 10**7, transcendentals=0),
            name='second',
        )(pin(positions), q_own, kn_own, vn_own, k3, v3, pin(k_rows), pin(v_rows))

        half_cols = d_model // 2
        cc = half_cols // OUT_CHUNKS
        chunk = pltpu.VMEM((OUT_CHUNKS, 2 * q4, cc), f32)
        h_out = pl.pallas_call(
            finish_kernel,
            out_shape=jax.ShapeDtypeStruct((n_seq, d_model), bf16),
            in_specs=[vm, hbm, vm, vm, vm, vm],
            out_specs=vm,
            scratch_shapes=[
                pltpu.VMEM((w_out.shape[0], half_cols), bf16),
                pltpu.VMEM((q4, n_q, head), f32),
                pltpu.VMEM((q4, n_q, head), f32),
                pltpu.VMEM((2 * q4, n_q * head), bf16),
                chunk, chunk, chunk, chunk, chunk, chunk,
                dma((OUT_CHUNKS,)), dma((2,)),
                dma((OUT_CHUNKS,)), dma((OUT_CHUNKS,)),
                dma((OUT_CHUNKS,)), dma((OUT_CHUNKS,)),
                dma((OUT_CHUNKS,)), dma((OUT_CHUNKS,)),
                dma((OUT_CHUNKS,)), dma((OUT_CHUNKS,)),
            ],
            compiler_params=pltpu.CompilerParams(
                collective_id=0, has_side_effects=True, vmem_limit_bytes=50 * 1024 * 1024),
            name='finish',
        )(hidden, pin(w_out), mine, got0, got1, got2)
        return h_out, k_upd.reshape(k_cache.shape), v_upd.reshape(v_cache.shape)

    return jax.shard_map(
        local_step,
        mesh=mesh,
        in_specs=(P('dp', None), P(None), P(None, 'tp'), P('tp', None), cache_spec, cache_spec, P('dp')),
        out_specs=(P('dp', None), cache_spec, cache_spec),
        check_vma=False,
    )
```

time: 162 us -> 43.5 us (0.27)
  waiting for transfers between devices: 65.7 us -> 0.01 us
  Pallas kernels: 0 us -> 38.4 us
  matrix products: 33.2 us -> 0 us
  other arithmetic: 24.1 us -> 0 us
  blocking collectives: 15 us -> 0 us
  between operations: 14.2 us -> 0.69 us
  local copies, waits for them, and re-layouts: 8.72 us -> 0.8 us
  starting transfers between devices: 0.08 us -> 3.51 us
    psum x2 -> x0, waiting for transfers between devices: 65.7 us -> none  [the longest x1 34.7 us: local_step(): proj_sum = lax.psum(head_part, 'tp')]
    pallas_call x0 -> x3, Pallas kernels: none -> 38.4 us  [the longest x1 16.2 us: local_step(): pl.pallas_call(finish_kernel, out_shape=jax.ShapeDtypeStruct((n_seq, d_mo...]
    dot_general x4 -> x0, matrix products: 33.2 us -> none  [the longest x1 12.9 us: local_step(): jnp.dot(normed, w_qkv, preferred_element_type=jnp.float32)]
    pmax x1 -> x0, blocking collectives: 15 us -> none  [local_step(): global_max = lax.pmax(local_max, 'sp')]
    select_n x1 -> x0, other arithmetic: 13.8 us -> none  [local_step(): v_upd = jnp.where(new_row, grouped[:, :, q_per_kv + 1][:, None], v_cache)]
    convert_element_type x5 -> x0, other arithmetic: 4.33 us -> none  [the longest x1 2.11 us: local_step(): h_out = (hidden_f32 + proj_sum).astype(jnp.bfloat16)]
    ppermute x0 -> x3, starting transfers between devices: none -> 3.51 us  [the longest x1 3.36 us: local_step(): got0 = lax.ppermute(pay0, 'sp', [(i, i ^ 2) for i in range(4)])]
    reduce_sum x3 -> x0, other arithmetic: 3.31 us -> none  [the longest x1 1.35 us: layer_norm_bf16(): row_var = jnp.mean(centered * centered, axis=-1, keepdims=True)]
  transfers between devices with their start and end apart: 2 -> 3, of which waited for: 2 -> 0; matrix products, arithmetic and copies ran while one was open for 0% -> 0% of each run, Pallas kernels for 0% -> 16%
where the time goes in v3:
time: 43.5 us; the launch traced here: 43.4 us
  Pallas kernels  38.4 us (88%)
  starting transfers between devices  3.51 us (8%)
  local copies, waits for them, and re-layouts  0.8 us (2%)
  between operations  0.69 us (2%)
    pallas_call x1, Pallas kernels, local_step(): pl.pallas_call(finish_kernel, out_shape=jax.ShapeDtypeStruct((n_seq, d_mo...  16.2 us
    pallas_call x1, Pallas kernels, local_step(): pl.pallas_call(first_kernel, out_shape=(pltpu.VMEM((3 * q4, rows, head),...  15.2 us
    pallas_call x1, Pallas kernels, local_step(): pl.pallas_call(second_kernel, out_shape=(jax.ShapeDtypeStruct((n_seq, row...  7.02 us
    ppermute x1, starting transfers between devices, local_step(): got0 = lax.ppermute(pay0, 'sp', [(i, i ^ 2) for i in range(4)])  3.36 us
  transfers between devices with their start and end apart: 3, of which 0 were waited for; matrix products, arithmetic and copies ran while one was open for 0% of the time, Pallas kernels for 16%

profile of v3, /device:TPU:0, one launch (start us, length us, event | category | flops | bytes accessed | tf_op | source)
XLA Modules:
  0.0 43.4 jit_solution(988249502808427569)
XLA Ops:
  0.6 15.2 %first.1 = (bf16[48,512,128]{2,1,0:T(8,128)(2,1)S(1)}, bf16[48,512,128]{2,1,0:T(8,128)(2,1)S(1)}, f32[17,16,128]{2,1,0:T(8,128)S(1)}, f32[17,16,128]{2,1,0:T(8,1...) custom-call(s32[64]{0:T(128)} %pos_hbm.3, ...), custom_call_target="tpu_custom_call" | custom-call | flops 20000000000 | bytes 40000000 | tf_op jit(solution)/shard_map/first/pallas_call | solution.py:376
  15.8 3.4 %collective-permute-start = (f32[17,16,128]{2,1,0:T(8,128)S(1)}, f32[17,16,128]{2,1,0:T(8,128)S(1)}, u32[]{:S(2)}, u32[]{:S(2)}) collective-permute-start(f32[17,16,128]{2,1,0:T(8,128)S(1)} %get-tuple-element.20), channel_id=1, source_target_pairs={{0,2},{1,3},{2,0},{3,1},{4,6},{5,7},{6,4},{7,5}} | collective-permute-start | bytes 417800 | tf_op jit(solution)/shard_map/ppermute | solution.py:403
  19.2 0.0 collective-permute-start.1
  19.2 0.1 collective-permute-start.2
  19.3 0.0 copy-start
  19.3 7.0 %second.1 = (bf16[64,512,128]{2,1,0:T(8,128)(2,1)}, bf16[64,512,128]{2,1,0:T(8,128)(2,1)}, f32[17,16,128]{2,1,0:T(8,128)S(1)}) custom-call(s32[64]{0:T(128)} %pos_hbm.3, f32[16,16,128]{2,1,0:T(8,128)S(1)} %get-tuple-element.14.q_ref, f32[16,16,128]{2,1,0:T(8,128)S(1)} %get-tuple-element.15.kn_ref, f32[16,16,128]{2,1,0:T(8,128)S(1)} %get-tuple-element.16.vn_ref, ...), custom_call_target="tpu_custom_call" | custom-call | flops 20000000000 | bytes 40000000 | tf_op jit(solution)/shard_map/second/pallas_call | solution.py:407
  26.4 0.0 collective-permute-done.p1_ref
  26.4 0.0 collective-permute-done.1.p2_ref
  26.4 0.0 collective-permute-done.2.p3_ref
  26.4 0.0 copy-done
  26.4 16.2 %finish.1 = bf16[64,4096]{1,0:T(8,128)(2,1)S(1)} custom-call(bf16[64,4096]{1,0:T(8,128)(2,1)S(1)} %copy-done, bf16[2048,4096]{1,0:T(8,128)(2,1)} %w_ref.3, f32[17,16,128]{2,1,0:T(8,128)S(1)} %get-tuple-element.19.p0_ref, f32[17,16,128]{2,1,0:T(8,128)S(1)} %collective-permute-done.p1_ref, f32[17,16,128]{2,1,0:T(8,128)S(1)} %collective-permute-done.1.p2_ref, ...), custom_call_target="tpu_custom_call" | custom-call | tf_op jit(solution)/shard_map/finish/pallas_call | solution.py:429
  42.6 0.8 %copy.11 = bf16[64,4096]{1,0:T(8,128)(2,1)} copy(bf16[64,4096]{1,0:T(8,128)(2,1)S(1)} %finish.1) | data formatting | bytes 1048576
Async XLA Ops:
  15.8 10.5 %collective-permute-start = (f32[17,16,128]{2,1,0:T(8,128)S(1)}, f32[17,16,128]{2,1,0:T(8,128)S(1)}, u32[]{:S(2)}, u32[]{:S(2)}) collective-permute-start(f32[17,16,128]{2,1,0:T(8,128)S(1)} %get-tuple-element.20), channel_id=1, source_target_pairs={{0,2},{1,3},{2,0},{3,1},{4,6},{5,7},{6,4},{7,5}} | collective-permute-start | bytes 417800 | tf_op jit(solution)/shard_map/ppermute | solution.py:403
  19.2 7.2 %collective-permute-start.1 = (f32[17,16,128]{2,1,0:T(8,128)S(1)}, f32[17,16,128]{2,1,0:T(8,128)S(1)}, u32[]{:S(2)}, u32[]{:S(2)}) collective-permute-start(f32[17,16,128]{2,1,0:T(8,128)S(1)} %get-tuple-element.21), channel_id=1, source_target_pairs={{0,3},{1,2},{2,1},{3,0},{4,7},{5,6},{6,5},{7,4}} | collective-permute-start | bytes 417800 | tf_op jit(solution)/shard_map/ppermute | solution.py:404
  19.2 7.2 %collective-permute-start.2 = (f32[17,16,128]{2,1,0:T(8,128)S(1)}, f32[17,16,128]{2,1,0:T(8,128)S(1)}, u32[]{:S(2)}, u32[]{:S(2)}) collective-permute-start(f32[17,16,128]{2,1,0:T(8,128)S(1)} %get-tuple-element.22), channel_id=1, source_target_pairs={{0,1},{1,0},{2,3},{3,2},{4,5},{5,4},{6,7},{7,6}} | collective-permute-start | bytes 417800 | tf_op jit(solution)/shard_map/ppermute | solution.py:405
  19.3 7.1 %copy-start = (bf16[64,4096]{1,0:T(8,128)(2,1)S(1)}, bf16[64,4096]{1,0:T(8,128)(2,1)}, u32[]{:S(2)}) copy-start(bf16[64,4096]{1,0:T(8,128)(2,1)} %h_ref.1) | copy-start | bytes 1572868

commit v4 on v3

--- a/solution.py
+++ b/solution.py
@@ -14,6 +14,7 @@
 PART = 8
 OUT_CHUNKS = 8
 LN_EPS = 1e-5
+FIRST_VMEM = 36
 
 
 def quarters(n_seq):
@@ -79,21 +80,23 @@
 
 
 def first_kernel(pos_hbm, h_hbm, scale_hbm, w_ref, kc_ref, vc_ref,
-                 k_ref, v_ref, pay0, pay1, pay2, q_own, kn_own, vn_own,
-                 pos_ref, h_ref, scale_ref, w_buf, u_ref, q_ref, kn_ref, vn_ref,
+                 k_ref, v_ref, pay0, pay1, pay2, q_own, kn_ref, vn_ref,
+                 pos_ref, h_ref, scale_ref, w_buf, u_ref, qkv_ref, q_ref,
                  ang_ref, idx_ref, s_ref,
-                 in_sem, w_sem, k_sem, v_sem):
+                 in_sem, w_sem, k_sem, v_sem, send_sem, recv_sem):
     n_seq, d_model = h_ref.shape
     rows = k_ref.shape[1]
     head = k_ref.shape[2]
-    kv_local = w_ref.shape[1] // (6 * head)
-    n_q = 4 * kv_local
-    base = lax.axis_index('sp') * (rows // kv_local)
+    w_chunks, _, w_cols = w_buf.shape
+    n_q = q_ref.shape[1]
+    kv_local = n_q // 4
+    sp = lax.axis_index('sp')
+    core = sp % 2
+    sib = {'sp': sp + 1 - 2 * core}
+    base = sp * (rows // kv_local)
     starts = quarters(n_seq)
     q4 = n_seq // 4
     per_slot = q4 // PART
-
-    w_chunks, _, w_cols = w_buf.shape
 
     small = [pltpu.make_async_copy(h_hbm, h_ref, in_sem.at[0]),
              pltpu.make_async_copy(scale_hbm, scale_ref, in_sem.at[1]),
@@ -102,7 +105,8 @@
         cp.start()
 
     def w_copy(t):
-        return pltpu.make_async_copy(w_ref.at[:, pl.ds(t * w_cols, w_cols)], w_buf.at[t], w_sem.at[t])
+        at = pl.multiple_of((core * w_chunks + t) * w_cols, 128)
+        return pltpu.make_async_copy(w_ref.at[:, pl.ds(at, w_cols)], w_buf.at[t], w_sem.at[t])
 
     def c_copies(i):
         src = pl.ds(starts[i // per_slot] + (i % per_slot) * PART, PART)
@@ -112,9 +116,12 @@
 
     for t in range(w_chunks):
         w_copy(t).start()
-    for i in range(3 * per_slot):
+    for i in range(4 * per_slot):
         for c in c_copies(i):
             c.start(priority=1)
+
+    barrier = pltpu.get_barrier_semaphore()
+    pl.semaphore_signal(barrier, inc=1, device_id=sib, device_id_type=MESH)
 
     idx_ref[...] = row_index(n_q, rows)
 
@@ -150,20 +157,31 @@
         cen = h_ref[:, i * 128:(i + 1) * 128].astype(jnp.float32) - mean
         u_ref[:, i * 128:(i + 1) * 128] = (
             cen * rstd * scale_ref[i:i + 1, :].astype(jnp.float32)).astype(jnp.bfloat16)
-
+    pl.semaphore_wait(barrier, 1)
+
+    heads = w_cols // head
+    sends = []
     for t in range(w_chunks):
         w_copy(t).wait()
         acc = jnp.dot(u_ref[...], w_buf[t], preferred_element_type=jnp.float32)
         qkv = jnp.clip(acc.astype(jnp.bfloat16).astype(jnp.float32), -8.0, 8.0)
-        for j in range(W_HEADS):
-            g, kind = divmod(t * W_HEADS + j, 6)
+        at = (core * w_chunks + t) * heads
+        for j in range(heads):
             val = qkv[:, j * head:(j + 1) * head]
-            if kind < 4:
-                q_ref[:, g * 4 + kind, :] = rope(val)
-                continue
-            new_ref, new = (kn_ref, rope(val)) if kind == 4 else (vn_ref, val)
-            for r in range(16 // kv_local):
-                new_ref[:, r * kv_local + g, :] = new
+            qkv_ref[at + j] = rope(val) if j % 6 < 5 else val
+        block = qkv_ref.at[pl.ds(at, heads)]
+        sends.append(pltpu.make_async_remote_copy(
+            src_ref=block, dst_ref=block, send_sem=send_sem.at[t], recv_sem=recv_sem.at[t],
+            device_id=sib, device_id_type=MESH))
+        sends[t].start()
+    for cp in sends:
+        cp.wait_recv()
+    for g in range(kv_local):
+        for j in range(4):
+            q_ref[:, g * 4 + j, :] = qkv_ref[g * 6 + j]
+        for r in range(16 // kv_local):
+            kn_ref[:, r * kv_local + g, :] = qkv_ref[g * 6 + 4]
+            vn_ref[:, r * kv_local + g, :] = qkv_ref[g * 6 + 5]
 
     pays = [pay0, pay1, pay2]
     lane_id = lax.broadcasted_iota(jnp.int32, (n_q, 128), 1)
@@ -175,91 +193,73 @@
     def arrive(i):
         for c in c_copies(i):
             c.wait()
-        for k in range(PART):
-            b = i * PART + k
-            insert_row(k_ref, v_ref, b, pos_ref[seq(b)] - base, kn_ref[seq(b)], vn_ref[seq(b)])
 
     def out_at(b, o, m, l):
         pays[b // q4][b % q4] = o
         stats[b // q4] = put_stats(stats[b // q4], lane_id, b % q4, m, l)
 
     parts = [list(range(i * PART, (i + 1) * PART)) for i in range(3 * per_slot)]
-    attend_parts(parts, arrive, lambda b: q_ref[seq(b)], lambda b: pos_ref[seq(b)] - base,
+    attend_parts(parts, arrive, lambda b: q_ref[seq(b)], lambda b: pos_ref[seq(b)] - base - 1,
                  k_ref, v_ref, idx_ref, s_ref, out_at)
     for pay, tile in zip(pays, stats):
         pay[q4] = tile
-    own = pl.ds(starts[3], q4)
-    q_own[...] = q_ref[own]
-    kn_own[...] = kn_ref[own]
-    vn_own[...] = vn_ref[own]
-
-
-def second_kernel(pos_hbm, q_ref, kn_ref, vn_ref, k3_ref, v3_ref, kc_ref, vc_ref,
-                  ko_ref, vo_ref, pay_ref,
-                  pos_ref, k_ref, v_ref, idx_ref, s_ref,
-                  in_sem, k_sem, v_sem, o_sem, o3_sem):
-    n_seq = ko_ref.shape[0]
-    rows = k_ref.shape[1]
+    q_own[...] = q_ref[pl.ds(starts[3], q4)]
+    for i in range(3 * per_slot, 4 * per_slot):
+        arrive(i)
+    for cp in sends:
+        cp.wait_send()
+
+
+def second_kernel(pos_hbm, q_ref, kn_ref, vn_ref, k_in, v_in,
+                  ko_ref, vo_ref, pay_ref, k_ref, v_ref,
+                  pos_ref, idx_ref, s_ref,
+                  in_sem, o_sem):
+    n_seq, rows, head = k_ref.shape
     n_q = q_ref.shape[1]
-    base = lax.axis_index('sp') * (rows // (n_q // 4))
+    kv_local = n_q // 4
+    base = lax.axis_index('sp') * (rows // kv_local)
     starts = quarters(n_seq)
     q4 = n_seq // 4
-    per_slot = q4 // PART
 
     pos_copy = pltpu.make_async_copy(pos_hbm, pos_ref, in_sem.at[0])
     pos_copy.start()
-
-    def c_copies(i):
-        src = pl.ds(starts[3] + i * PART, PART)
-        dst = pl.ds(i * PART, PART)
-        return (pltpu.make_async_copy(kc_ref.at[src], k_ref.at[dst], k_sem.at[i]),
-                pltpu.make_async_copy(vc_ref.at[src], v_ref.at[dst], v_sem.at[i]))
+    idx_ref[...] = row_index(n_q, rows)
+    pos_copy.wait()
 
     def o_copies(i):
-        dst = pl.ds(starts[3] + i * PART, PART)
-        src = pl.ds(i * PART, PART)
+        dst = pl.ds(starts[i], q4)
+        src = pl.ds(i * q4, q4)
         return (pltpu.make_async_copy(k_ref.at[src], ko_ref.at[dst], o_sem.at[0, i]),
                 pltpu.make_async_copy(v_ref.at[src], vo_ref.at[dst], o_sem.at[1, i]))
 
-    def o3_copies(i):
-        dst = pl.ds(starts[i], q4)
-        src = pl.ds(i * q4, q4)
-        return (pltpu.make_async_copy(k3_ref.at[src], ko_ref.at[dst], o3_sem.at[0, i]),
-                pltpu.make_async_copy(v3_ref.at[src], vo_ref.at[dst], o3_sem.at[1, i]))
-
-    for i in range(per_slot):
-        for c in c_copies(i):
+    for i in range(4):
+        for k in range(q4):
+            b = starts[i] + k
+            insert_row(k_ref, v_ref, i * q4 + k, pos_ref[b] - base, kn_ref[b], vn_ref[b])
+        for c in o_copies(i):
             c.start()
-    for i in range(3):
-        for c in o3_copies(i):
-            c.start(priority=1)
-    idx_ref[...] = row_index(n_q, rows)
-    pos_copy.wait()
 
     lane_id = lax.broadcasted_iota(jnp.int32, (n_q, 128), 1)
     stats = [jnp.zeros((n_q, 128), jnp.float32)]
 
-    def arrive(i):
-        for c in c_copies(i):
-            c.wait()
-        for k in range(PART):
-            b = i * PART + k
-            insert_row(k_ref, v_ref, b, pos_ref[starts[3] + b] - base, kn_ref[b], vn_ref[b])
-        for c in o_copies(i):
-            c.start(priority=1)
+    def per_head(tile):
+        return jnp.concatenate([jnp.broadcast_to(tile[g:g + 1], (4, head)) for g in range(kv_local)], axis=0)
 
     def out_at(b, o, m, l):
-        pay_ref[b] = o
-        stats[0] = put_stats(stats[0], lane_id, b, m, l)
-
-    parts = [list(range(i * PART, (i + 1) * PART)) for i in range(per_slot)]
-    attend_parts(parts, arrive, lambda b: q_ref[b], lambda b: pos_ref[starts[3] + b] - base,
+        k = b - 3 * q4
+        at = starts[3] + k
+        s = jnp.sum(q_ref[k] * per_head(kn_ref[at]), axis=1, keepdims=True) * head ** -0.5
+        top = jnp.maximum(m, s)
+        old, new = jnp.exp(m - top), jnp.exp(s - top)
+        pay_ref[k] = o * old + new.astype(jnp.bfloat16).astype(jnp.float32) * per_head(vn_ref[at])
+        stats[0] = put_stats(stats[0], lane_id, k, top, l * old + new)
+
+    parts = [list(range(3 * q4 + i, 3 * q4 + i + PART)) for i in range(0, q4, PART)]
+    attend_parts(parts, lambda i: None, lambda b: q_ref[b - 3 * q4],
+                 lambda b: pos_ref[starts[3] + b - 3 * q4] - base - 1,
                  k_ref, v_ref, idx_ref, s_ref, out_at)
     pay_ref[q4] = stats[0]
-    for i in range(3):
-        for c in o3_copies(i):
-            c.wait()
-    for i in range(per_slot):
+    for i in range(4):
         for c in o_copies(i):
             c.wait()
 
@@ -368,34 +368,35 @@
         payload = pltpu.VMEM((q4 + 1, n_q, head), f32)
         k_rows = k_cache.reshape(n_seq, rows, head)
         v_rows = v_cache.reshape(n_seq, rows, head)
-        slots = 3 * q4 // PART
+        slots = n_seq // PART
 
         def pin(a):
             return pltpu.with_memory_space_constraint(a, pltpu.HBM)
 
-        k3, v3, pay0, pay1, pay2, q_own, kn_own, vn_own = pl.pallas_call(
+        k_all, v_all, pay0, pay1, pay2, q_own, kn, vn = pl.pallas_call(
             first_kernel,
-            out_shape=(pltpu.VMEM((3 * q4, rows, head), bf16), pltpu.VMEM((3 * q4, rows, head), bf16),
+            out_shape=(pltpu.VMEM((n_seq, rows, head), bf16), pltpu.VMEM((n_seq, rows, head), bf16),
                        payload, payload, payload,
-                       pltpu.VMEM((q4, n_q, head), f32), pltpu.VMEM((q4, 16, head), f32),
-                       pltpu.VMEM((q4, 16, head), f32)),
+                       pltpu.VMEM((q4, n_q, head), f32), pltpu.VMEM((n_seq, 16, head), f32),
+                       pltpu.VMEM((n_seq, 16, head), f32)),
             in_specs=[hbm] * 6,
             out_specs=(vm,) * 8,
             scratch_shapes=[
                 pltpu.SMEM((n_seq,), jnp.int32),
                 pltpu.VMEM((n_seq, d_model), bf16),
                 pltpu.VMEM((d_model // 128, 128), bf16),
-                pltpu.VMEM((6 * kv_local // W_HEADS, d_model, W_HEADS * head), bf16),
+                pltpu.VMEM((3 * kv_local // W_HEADS, d_model, W_HEADS * head), bf16),
                 pltpu.VMEM((n_seq, d_model), bf16),
+                pltpu.VMEM((6 * kv_local, n_seq, head), f32),
                 pltpu.VMEM((n_seq, n_q, head), f32),
-                pltpu.VMEM((n_seq, 16, head), f32),
-                pltpu.VMEM((n_seq, 16, head), f32),
                 pltpu.VMEM((n_seq, head), f32),
                 pltpu.VMEM((n_q, rows), jnp.int32),
                 pltpu.VMEM((2, PART, n_q, rows), f32),
-                dma((3,)), dma((6 * kv_local // W_HEADS,)), dma((slots,)), dma((slots,)),
+                dma((3,)), dma((3 * kv_local // W_HEADS,)), dma((slots,)), dma((slots,)),
+                dma((3 * kv_local // W_HEADS,)), dma((3 * kv_local // W_HEADS,)),
             ],
-            compiler_params=pltpu.CompilerParams(vmem_limit_bytes=40 * 1024 * 1024),
+            compiler_params=pltpu.CompilerParams(
+                collective_id=1, has_side_effects=True, vmem_limit_bytes=FIRST_VMEM * 1024 * 1024),
             cost_estimate=pl.CostEstimate(flops=2 * 10**10, bytes_accessed=4 * 10**7, transcendentals=0),
             name='first',
         )(*map(pin, (positions, hidden, norm_scale.reshape(d_model // 128, 128), w_qkv, k_rows, v_rows)))
@@ -404,24 +405,24 @@
         got1 = lax.ppermute(pay1, 'sp', [(i, 3 - i) for i in range(4)])
         got2 = lax.ppermute(pay2, 'sp', [(i, i ^ 1) for i in range(4)])
 
-        k_upd, v_upd, mine = pl.pallas_call(
+        k_upd, v_upd, mine, _, _ = pl.pallas_call(
             second_kernel,
             out_shape=(jax.ShapeDtypeStruct((n_seq, rows, head), bf16),
-                       jax.ShapeDtypeStruct((n_seq, rows, head), bf16), payload),
-            in_specs=[hbm, vm, vm, vm, vm, vm, hbm, hbm],
-            out_specs=(hbm, hbm, vm),
+                       jax.ShapeDtypeStruct((n_seq, rows, head), bf16), payload,
+                       pltpu.VMEM((n_seq, rows, head), bf16), pltpu.VMEM((n_seq, rows, head), bf16)),
+            in_specs=[hbm, vm, vm, vm, vm, vm],
+            out_specs=(hbm, hbm, vm, vm, vm),
+            input_output_aliases={4: 3, 5: 4},
             scratch_shapes=[
                 pltpu.SMEM((n_seq,), jnp.int32),
-                pltpu.VMEM((q4, rows, head), bf16),
-                pltpu.VMEM((q4, rows, head), bf16),
                 pltpu.VMEM((n_q, rows), jnp.int32),
                 pltpu.VMEM((2, PART, n_q, rows), f32),
-                dma((1,)), dma((q4 // PART,)), dma((q4 // PART,)), dma((2, q4 // PART)), dma((2, 3)),
+                dma((1,)), dma((2, 4)),
             ],
-            compiler_params=pltpu.CompilerParams(vmem_limit_bytes=40 * 1024 * 1024),
+            compiler_params=pltpu.CompilerParams(vmem_limit_bytes=FIRST_VMEM * 1024 * 1024),
             cost_estimate=pl.CostEstimate(flops=2 * 10**10, bytes_accessed=4 * 10**7, transcendentals=0),
             name='second',
-        )(pin(positions), q_own, kn_own, vn_own, k3, v3, pin(k_rows), pin(v_rows))
+        )(pin(positions), q_own, kn, vn, k_all, v_all)
 
         half_cols = d_model // 2
         cc = half_cols // OUT_CHUNKS

time: 43.5 us -> 39.7 us (0.913)
  Pallas kernels: 38.4 us -> 35.2 us
  starting transfers between devices: 3.51 us -> 2.74 us
    pallas_call x1, Pallas kernels: 15.2 us -> 12.6 us  [local_step(): pl.pallas_call(first_kernel, out_shape=(pltpu.VMEM((n_seq, rows, head), b...]
    ppermute x1, starting transfers between devices: 3.36 us -> 2.34 us  [local_step(): got0 = lax.ppermute(pay0, 'sp', [(i, i ^ 2) for i in range(4)])]
  transfers between devices with their start and end apart: 3 -> 3, of which waited for: 0 -> 1; matrix products, arithmetic and copies ran while one was open for 0% -> 0% of each run, Pallas kernels for 16% -> 17%
where the time goes in v4:
time: 39.7 us; the launch traced here: 39.6 us
  Pallas kernels  35.2 us (89%)
  starting transfers between devices  2.74 us (7%)
  local copies, waits for them, and re-layouts  0.8 us (2%)
  between operations  0.67 us (2%)
    pallas_call x1, Pallas kernels, local_step(): pl.pallas_call(finish_kernel, out_shape=jax.ShapeDtypeStruct((n_seq, d_mo...  15.8 us
    pallas_call x1, Pallas kernels, local_step(): pl.pallas_call(first_kernel, out_shape=(pltpu.VMEM((n_seq, rows, head), b...  12.6 us
    pallas_call x1, Pallas kernels, local_step(): pl.pallas_call(second_kernel, out_shape=(jax.ShapeDtypeStruct((n_seq, row...  6.86 us
    ppermute x1, starting transfers between devices, local_step(): got0 = lax.ppermute(pay0, 'sp', [(i, i ^ 2) for i in range(4)])  2.34 us
    unnamed x3, local copies, waits for them, and re-layouts  0.8 us
  transfers between devices with their start and end apart: 3, of which 1 were waited for; matrix products, arithmetic and copies ran while one was open for 0% of the time, Pallas kernels for 17%

profile of v4, /device:TPU:0, one launch (start us, length us, event | category | flops | bytes accessed | tf_op | source)
XLA Modules:
  0.0 39.6 jit_solution(16548447700245572702)
XLA Ops:
  0.6 12.6 %first.1 = (bf16[64,512,128]{2,1,0:T(8,128)(2,1)S(1)}, bf16[64,512,128]{2,1,0:T(8,128)(2,1)S(1)}, f32[17,16,128]{2,1,0:T(8,128)S(1)}, f32[17,16,128]{2,1,0:T(8,1...) custom-call(s32[64]{0:T(128)} %pos_hbm.3, ...), custom_call_target="tpu_custom_call" | custom-call | flops 20000000000 | bytes 40000000 | tf_op jit(solution)/shard_map/first/pallas_call | solution.py:376
  13.2 2.3 %collective-permute-start = (f32[17,16,128]{2,1,0:T(8,128)S(1)}, f32[17,16,128]{2,1,0:T(8,128)S(1)}, u32[]{:S(2)}, u32[]{:S(2)}) collective-permute-start(f32[17,16,128]{2,1,0:T(8,128)S(1)} %get-tuple-element.20), channel_id=1, source_target_pairs={{0,2},{1,3},{2,0},{3,1},{4,6},{5,7},{6,4},{7,5}} | collective-permute-start | bytes 417800 | tf_op jit(solution)/shard_map/ppermute | solution.py:404
  15.6 0.3 collective-permute-start.1
  15.9 0.1 collective-permute-start.2
  16.0 0.0 copy-start
  16.0 6.9 %second.1 = (bf16[64,512,128]{2,1,0:T(8,128)(2,1)}, bf16[64,512,128]{2,1,0:T(8,128)(2,1)}, f32[17,16,128]{2,1,0:T(8,128)S(1)}, bf16[64,512,128]{2,1,0:T(8,128)(2,1)S(1)}, bf16[64,512,128]{2,1,0:T(8,128)(2,1)S(1)}) custom-call(s32[64]{0:T(128)} %pos_hbm.3, f32[16,16,128]{2,1,0:T(8,128)S(1)} %get-tuple-element.14.q_ref, ...), custom_call_target="tpu_custom_call", output_to_operand_aliasing={{3}: (4, {}), {4}: (5, {})} | custom-call | flops 20000000000 | bytes 40000000 | tf_op jit(solution)/shard_map/second/pallas_call | solution.py:408
  22.8 0.0 collective-permute-done.p1_ref
  22.8 0.2 collective-permute-done.1.p2_ref
  23.0 0.0 collective-permute-done.2.p3_ref
  23.0 0.0 copy-done
  23.0 15.8 %finish.1 = bf16[64,4096]{1,0:T(8,128)(2,1)S(1)} custom-call(bf16[64,4096]{1,0:T(8,128)(2,1)S(1)} %copy-done, bf16[2048,4096]{1,0:T(8,128)(2,1)} %w_ref.3, f32[17,16,128]{2,1,0:T(8,128)S(1)} %get-tuple-element.19.p0_ref, f32[17,16,128]{2,1,0:T(8,128)S(1)} %collective-permute-done.p1_ref, f32[17,16,128]{2,1,0:T(8,128)S(1)} %collective-permute-done.1.p2_ref, ...), custom_call_target="tpu_custom_call" | custom-call | tf_op jit(solution)/shard_map/finish/pallas_call | solution.py:430
  38.8 0.8 %copy.15 = bf16[64,4096]{1,0:T(8,128)(2,1)} copy(bf16[64,4096]{1,0:T(8,128)(2,1)S(1)} %finish.1) | data formatting | bytes 1048576
Async XLA Ops:
  13.2 9.6 %collective-permute-start = (f32[17,16,128]{2,1,0:T(8,128)S(1)}, f32[17,16,128]{2,1,0:T(8,128)S(1)}, u32[]{:S(2)}, u32[]{:S(2)}) collective-permute-start(f32[17,16,128]{2,1,0:T(8,128)S(1)} %get-tuple-element.20), channel_id=1, source_target_pairs={{0,2},{1,3},{2,0},{3,1},{4,6},{5,7},{6,4},{7,5}} | collective-permute-start | bytes 417800 | tf_op jit(solution)/shard_map/ppermute | solution.py:404
  15.6 7.5 %collective-permute-start.1 = (f32[17,16,128]{2,1,0:T(8,128)S(1)}, f32[17,16,128]{2,1,0:T(8,128)S(1)}, u32[]{:S(2)}, u32[]{:S(2)}) collective-permute-start(f32[17,16,128]{2,1,0:T(8,128)S(1)} %get-tuple-element.21), channel_id=1, source_target_pairs={{0,3},{1,2},{2,1},{3,0},{4,7},{5,6},{6,5},{7,4}} | collective-permute-start | bytes 417800 | tf_op jit(solution)/shard_map/ppermute | solution.py:405
  15.9 7.2 %collective-permute-start.2 = (f32[17,16,128]{2,1,0:T(8,128)S(1)}, f32[17,16,128]{2,1,0:T(8,128)S(1)}, u32[]{:S(2)}, u32[]{:S(2)}) collective-permute-start(f32[17,16,128]{2,1,0:T(8,128)S(1)} %get-tuple-element.22), channel_id=1, source_target_pairs={{0,1},{1,0},{2,3},{3,2},{4,5},{5,4},{6,7},{7,6}} | collective-permute-start | bytes 417800 | tf_op jit(solution)/shard_map/ppermute | solution.py:406
  16.0 7.1 %copy-start = (bf16[64,4096]{1,0:T(8,128)(2,1)S(1)}, bf16[64,4096]{1,0:T(8,128)(2,1)}, u32[]{:S(2)}) copy-start(bf16[64,4096]{1,0:T(8,128)(2,1)} %h_ref.1) | copy-start | bytes 1572868

commit v5 on v4

--- a/solution.py
+++ b/solution.py
@@ -10,8 +10,9 @@
 MESH = pl.DeviceIdType.MESH
 NEG = -1e30
 PV_LAG = 4
-W_HEADS = 6
+W_HEADS = 4
 PART = 8
+EARLY_PARTS = 6
 OUT_CHUNKS = 8
 LN_EPS = 1e-5
 FIRST_VMEM = 36
@@ -24,7 +25,8 @@
 
     def start(xx, cc):
         return pl.multiple_of((xx * 2 + cc) * q, q)
-    return [start(1 - x, c), start(1 - x, 1 - c), start(x, 1 - c), start(x, c)]
+    own = start(x, 0)
+    return [start(1 - x, 1 - c), start(1 - x, c), own, pl.multiple_of(own + q, q)]
 
 
 def insert_row(k_ref, v_ref, at_b, p, kn, vn):
@@ -36,6 +38,21 @@
     hit = lax.broadcasted_iota(jnp.int32, (16, head), 0) // kv_local == p - tile * per
     k_ref[at_b, at, :] = jnp.where(hit, kn, k_ref[at_b, at, :].astype(jnp.float32)).astype(jnp.bfloat16)
     v_ref[at_b, at, :] = jnp.where(hit, vn, v_ref[at_b, at, :].astype(jnp.float32)).astype(jnp.bfloat16)
+
+
+def write_copies(i, starts, q4, k_ref, v_ref, ko_ref, vo_ref, sem, first=0):
+    at = i * PART
+    src = pl.ds(at - first * PART, PART)
+    dst = pl.ds(starts[at // q4] + at % q4, PART)
+    return (pltpu.make_async_copy(k_ref.at[src], ko_ref.at[dst], sem.at[0, i]),
+            pltpu.make_async_copy(v_ref.at[src], vo_ref.at[dst], sem.at[1, i]))
+
+
+def insert_part(i, starts, base, pos_ref, k_ref, v_ref, kn_ref, vn_ref):
+    q4 = k_ref.shape[0] // 4
+    for k in range(i * PART, (i + 1) * PART):
+        b = starts[k // q4] + k % q4
+        insert_row(k_ref, v_ref, k, pos_ref[b] - base, kn_ref[b], vn_ref[b])
 
 
 def row_index(n_q, rows):
@@ -80,9 +97,9 @@
 
 
 def first_kernel(pos_hbm, h_hbm, scale_hbm, w_ref, kc_ref, vc_ref,
-                 k_ref, v_ref, pay0, pay1, pay2, q_own, kn_ref, vn_ref,
+                 k_ref, v_ref, pay_ref, q_own, kn_ref, vn_ref,
                  pos_ref, h_ref, scale_ref, w_buf, u_ref, qkv_ref, q_ref,
-                 ang_ref, idx_ref, s_ref,
+                 ang_ref, idx_ref, s_ref, out_pay, sib_pay,
                  in_sem, w_sem, k_sem, v_sem, send_sem, recv_sem):
     n_seq, d_model = h_ref.shape
     rows = k_ref.shape[1]
@@ -116,9 +133,6 @@
 
     for t in range(w_chunks):
         w_copy(t).start()
-    for i in range(4 * per_slot):
-        for c in c_copies(i):
-            c.start(priority=1)
 
     barrier = pltpu.get_barrier_semaphore()
     pl.semaphore_signal(barrier, inc=1, device_id=sib, device_id_type=MESH)
@@ -163,12 +177,16 @@
     sends = []
     for t in range(w_chunks):
         w_copy(t).wait()
+        if t == 0:
+            for i in range(4 * per_slot):
+                for c in c_copies(i):
+                    c.start(priority=1)
         acc = jnp.dot(u_ref[...], w_buf[t], preferred_element_type=jnp.float32)
         qkv = jnp.clip(acc.astype(jnp.bfloat16).astype(jnp.float32), -8.0, 8.0)
         at = (core * w_chunks + t) * heads
         for j in range(heads):
             val = qkv[:, j * head:(j + 1) * head]
-            qkv_ref[at + j] = rope(val) if j % 6 < 5 else val
+            qkv_ref[at + j] = rope(val) if (t * heads + j) % 6 < 5 else val
         block = qkv_ref.at[pl.ds(at, heads)]
         sends.append(pltpu.make_async_remote_copy(
             src_ref=block, dst_ref=block, send_sem=send_sem.at[t], recv_sem=recv_sem.at[t],
@@ -179,13 +197,13 @@
     for g in range(kv_local):
         for j in range(4):
             q_ref[:, g * 4 + j, :] = qkv_ref[g * 6 + j]
-        for r in range(16 // kv_local):
-            kn_ref[:, r * kv_local + g, :] = qkv_ref[g * 6 + 4]
-            vn_ref[:, r * kv_local + g, :] = qkv_ref[g * 6 + 5]
-
-    pays = [pay0, pay1, pay2]
+
     lane_id = lax.broadcasted_iota(jnp.int32, (n_q, 128), 1)
+    pays = [out_pay, pay_ref]
     stats = [jnp.zeros((n_q, 128), jnp.float32) for _ in pays]
+    pay_copy = pltpu.make_async_remote_copy(
+        src_ref=out_pay, dst_ref=sib_pay, send_sem=send_sem.at[w_chunks], recv_sem=recv_sem.at[w_chunks],
+        device_id=sib, device_id_type=MESH)
 
     def seq(b):
         return starts[b // q4] + b % q4
@@ -195,29 +213,47 @@
             c.wait()
 
     def out_at(b, o, m, l):
-        pays[b // q4][b % q4] = o
-        stats[b // q4] = put_stats(stats[b // q4], lane_id, b % q4, m, l)
-
-    parts = [list(range(i * PART, (i + 1) * PART)) for i in range(3 * per_slot)]
+        if b < 2 * kv_local:
+            g, new_ref = b // 2, (kn_ref, vn_ref)[b % 2]
+            for r in range(16 // kv_local):
+                new_ref[:, r * kv_local + g, :] = qkv_ref[g * 6 + 4 + b % 2]
+        slot = b // q4
+        pays[slot][b % q4] = o
+        stats[slot] = put_stats(stats[slot], lane_id, b % q4, m, l)
+        if b == q4 - 1:
+            out_pay[q4] = stats[0]
+            pay_copy.start()
+
+    parts = [list(range(i * PART, (i + 1) * PART)) for i in range(2 * per_slot)]
     attend_parts(parts, arrive, lambda b: q_ref[seq(b)], lambda b: pos_ref[seq(b)] - base - 1,
                  k_ref, v_ref, idx_ref, s_ref, out_at)
-    for pay, tile in zip(pays, stats):
-        pay[q4] = tile
-    q_own[...] = q_ref[pl.ds(starts[3], q4)]
-    for i in range(3 * per_slot, 4 * per_slot):
+
+    pay_copy.wait_recv()
+    other = sib_pay[q4]
+    top = jnp.maximum(stats[1], other)
+    f0, f1 = jnp.exp(stats[1] - top), jnp.exp(other - top)
+    total = pltpu.roll(stats[1], 64, 1) * f0 + pltpu.roll(other, 64, 1) * f1
+    pay_ref[q4] = jnp.where(lane_id < 64, top, pltpu.roll(total, 64, 1))
+    for i in range(q4):
+        pay_ref[i] = (pay_ref[i] * jnp.broadcast_to(f0[:, i:i + 1], (n_q, 128))
+                      + sib_pay[i] * jnp.broadcast_to(f1[:, i:i + 1], (n_q, 128)))
+    q_own[...] = q_ref[pl.ds(starts[2], 2 * q4)]
+    for i in range(2 * per_slot, 4 * per_slot):
         arrive(i)
-    for cp in sends:
+    for cp in sends + [pay_copy]:
         cp.wait_send()
 
 
-def second_kernel(pos_hbm, q_ref, kn_ref, vn_ref, k_in, v_in,
-                  ko_ref, vo_ref, pay_ref, k_ref, v_ref,
+def second_kernel(pos_hbm, q_ref, kn_ref, vn_ref, k_ref, v_ref,
+                  ko_ref, vo_ref, pay_ref, k_late, v_late,
                   pos_ref, idx_ref, s_ref,
                   in_sem, o_sem):
     n_seq, rows, head = k_ref.shape
-    n_q = q_ref.shape[1]
+    half_seq, n_q = q_ref.shape[:2]
     kv_local = n_q // 4
-    base = lax.axis_index('sp') * (rows // kv_local)
+    sp = lax.axis_index('sp')
+    core = sp % 2
+    base = sp * (rows // kv_local)
     starts = quarters(n_seq)
     q4 = n_seq // 4
 
@@ -226,18 +262,18 @@
     idx_ref[...] = row_index(n_q, rows)
     pos_copy.wait()
 
-    def o_copies(i):
-        dst = pl.ds(starts[i], q4)
-        src = pl.ds(i * q4, q4)
-        return (pltpu.make_async_copy(k_ref.at[src], ko_ref.at[dst], o_sem.at[0, i]),
-                pltpu.make_async_copy(v_ref.at[src], vo_ref.at[dst], o_sem.at[1, i]))
-
-    for i in range(4):
-        for k in range(q4):
-            b = starts[i] + k
-            insert_row(k_ref, v_ref, i * q4 + k, pos_ref[b] - base, kn_ref[b], vn_ref[b])
-        for c in o_copies(i):
+    for i in range(EARLY_PARTS):
+        insert_part(i, starts, base, pos_ref, k_ref, v_ref, kn_ref, vn_ref)
+        for c in write_copies(i, starts, q4, k_ref, v_ref, ko_ref, vo_ref, o_sem):
             c.start()
+
+    late = EARLY_PARTS * PART
+
+    def late_row(k):
+        k_late[k - late] = k_ref[k]
+        v_late[k - late] = v_ref[k]
+        b = starts[k // q4] + k % q4
+        insert_row(k_late, v_late, k - late, pos_ref[b] - base, kn_ref[b], vn_ref[b])
 
     lane_id = lax.broadcasted_iota(jnp.int32, (n_q, 128), 1)
     stats = [jnp.zeros((n_q, 128), jnp.float32)]
@@ -246,28 +282,44 @@
         return jnp.concatenate([jnp.broadcast_to(tile[g:g + 1], (4, head)) for g in range(kv_local)], axis=0)
 
     def out_at(b, o, m, l):
-        k = b - 3 * q4
-        at = starts[3] + k
+        k = b - half_seq
+        at = starts[2] + k
         s = jnp.sum(q_ref[k] * per_head(kn_ref[at]), axis=1, keepdims=True) * head ** -0.5
+        s = jnp.where(core == k // q4, s, NEG)
         top = jnp.maximum(m, s)
-        old, new = jnp.exp(m - top), jnp.exp(s - top)
+        old = jnp.exp(m - top)
+        new = jnp.where(core == k // q4, jnp.exp(s - top), 0.0)
         pay_ref[k] = o * old + new.astype(jnp.bfloat16).astype(jnp.float32) * per_head(vn_ref[at])
         stats[0] = put_stats(stats[0], lane_id, k, top, l * old + new)
-
-    parts = [list(range(3 * q4 + i, 3 * q4 + i + PART)) for i in range(0, q4, PART)]
-    attend_parts(parts, lambda i: None, lambda b: q_ref[b - 3 * q4],
-                 lambda b: pos_ref[starts[3] + b - 3 * q4] - base - 1,
+        if b >= late:
+            late_row(b)
+
+    parts = [list(range(half_seq + i, half_seq + i + PART)) for i in range(0, half_seq, PART)]
+    attend_parts(parts, lambda i: None, lambda b: q_ref[b - half_seq],
+                 lambda b: pos_ref[starts[2] + b - half_seq] - base - 1,
                  k_ref, v_ref, idx_ref, s_ref, out_at)
-    pay_ref[q4] = stats[0]
-    for i in range(4):
-        for c in o_copies(i):
+    pay_ref[half_seq] = stats[0]
+    for i in range(EARLY_PARTS):
+        for c in write_copies(i, starts, q4, k_ref, v_ref, ko_ref, vo_ref, o_sem):
             c.wait()
 
 
-def finish_kernel(h_ref, w_ref, p0_ref, p1_ref, p2_ref, p3_ref, out_ref,
-                  w_buf, att, att_send, lhs, part, y_in, fin, x_in, d_in, d_in2,
-                  w_sem, a_sem, ys_sem, yr_sem, xs_sem, xr_sem, ds_sem, dr_sem, es_sem, er_sem):
-    n_q = p0_ref.shape[1]
+def third_kernel(k_late, v_late, k_in, v_in, ko_ref, vo_ref, o_sem):
+    n_seq = ko_ref.shape[0]
+    starts = quarters(n_seq)
+    parts = range(EARLY_PARTS, n_seq // PART)
+    for i in parts:
+        for c in write_copies(i, starts, n_seq // 4, k_late, v_late, ko_ref, vo_ref, o_sem, EARLY_PARTS):
+            c.start()
+    for i in parts:
+        for c in write_copies(i, starts, n_seq // 4, k_late, v_late, ko_ref, vo_ref, o_sem, EARLY_PARTS):
+            c.wait()
+
+
+def finish_kernel(h_ref, w_ref, mine_ref, sib_ref, got_ref, sib_got_ref, out_ref,
+                  w_buf, att, got2, lhs, part, y_in, fin, x_in, d_in, d_in2,
+                  w_sem, ys_sem, yr_sem, xs_sem, xr_sem, ds_sem, dr_sem, es_sem, er_sem):
+    n_q = mine_ref.shape[1]
     sp = lax.axis_index('sp')
     tp = lax.axis_index('tp')
     x, c = sp // 2, sp % 2
@@ -277,7 +329,7 @@
 
     half_cols = w_buf.shape[1]
     cc = half_cols // OUT_CHUNKS
-    q4 = att_send.shape[0]
+    q4 = got_ref.shape[0] - 1
     own_col = c * half_cols
     oth_col = (1 - c) * half_cols
 
@@ -297,29 +349,30 @@
         return pltpu.make_async_remote_copy(src_ref=src, dst_ref=dst, send_sem=ssem, recv_sem=rsem,
                                             device_id=dev, device_id_type=MESH)
 
-    pays = [p0_ref, p1_ref, p2_ref, p3_ref]
-    maxes = [p[q4] for p in pays]
+    got2[c] = got_ref[...]
+    got2[1 - c] = sib_got_ref[...]
+
+    lane_id = lax.broadcasted_iota(jnp.int32, (n_q, 128), 1)
+    far = got2[1, q4]
+    far = jnp.where(lane_id % 64 < q4, got2[0, q4], pltpu.roll(far, q4, 1))
+    maxes = [mine_ref[2 * q4], sib_ref[2 * q4], far]
     sums = [pltpu.roll(m, 64, 1) for m in maxes]
-    top = jnp.maximum(jnp.maximum(maxes[0], maxes[1]), jnp.maximum(maxes[2], maxes[3]))
+    top = jnp.maximum(jnp.maximum(maxes[0], maxes[1]), maxes[2])
     factors = [jnp.exp(m - top) for m in maxes]
-    inv = 1.0 / sum(l * f for l, f in zip(sums, factors))
+    inv = 1.0 / (sums[0] * factors[0] + sums[1] * factors[1] + sums[2] * factors[2])
     factors = [f * inv for f in factors]
-    for i in range(q4):
-        att_send[i] = sum(p[i] * jnp.broadcast_to(f[:, i:i + 1], (n_q, 128)) for p, f in zip(pays, factors))
-
-    pl.semaphore_wait(barrier, 3)
-    c_att = remote(att_send, att, a_sem.at[0], a_sem.at[1], sib)
-    c_att.start()
+    for i in range(2 * q4):
+        f0, f1, f2 = (jnp.broadcast_to(f[:, i:i + 1], (n_q, 128)) for f in factors)
+        att[i] = mine_ref[i] * f0 + sib_ref[i] * f1 + got2[i // q4, i % q4] * f2
     for n in range(n_q):
-        lhs[pl.ds(c * q4, q4), n * 128:(n + 1) * 128] = att_send[:, n, :].astype(jnp.bfloat16)
-    c_att.wait_recv()
-    for n in range(n_q):
-        lhs[pl.ds((1 - c) * q4, q4), n * 128:(n + 1) * 128] = att[:, n, :].astype(jnp.bfloat16)
+        lhs[:, n * 128:(n + 1) * 128] = att[:, n, :].astype(jnp.bfloat16)
 
     y_copy, x_copy, d_copy, e_copy = [], [], [], []
     for j in range(OUT_CHUNKS):
         w_copy(j).wait()
         part[j] = jnp.dot(lhs[...], w_buf[:, j * cc:(j + 1) * cc], preferred_element_type=jnp.float32)
+        if j == 0:
+            pl.semaphore_wait(barrier, 3)
         y_copy.append(remote(part.at[j], y_in.at[j], ys_sem.at[j], yr_sem.at[j], yn))
         y_copy[j].start()
 
@@ -348,7 +401,7 @@
         e_copy[j].wait_recv()
         out_ref[xn_rows, cols(oth_col, j)] = d_in2[j].astype(jnp.bfloat16)
 
-    for cp in [c_att] + y_copy + x_copy + d_copy + e_copy:
+    for cp in y_copy + x_copy + d_copy + e_copy:
         cp.wait_send()
 
 
@@ -366,34 +419,38 @@
         dma = pltpu.SemaphoreType.DMA
         f32, bf16 = jnp.float32, jnp.bfloat16
         payload = pltpu.VMEM((q4 + 1, n_q, head), f32)
+        payload2 = pltpu.VMEM((2 * q4 + 1, n_q, head), f32)
         k_rows = k_cache.reshape(n_seq, rows, head)
         v_rows = v_cache.reshape(n_seq, rows, head)
         slots = n_seq // PART
+        late = pltpu.VMEM((n_seq - EARLY_PARTS * PART, rows, head), bf16)
+        w_chunks = 3 * kv_local // W_HEADS
 
         def pin(a):
             return pltpu.with_memory_space_constraint(a, pltpu.HBM)
 
-        k_all, v_all, pay0, pay1, pay2, q_own, kn, vn = pl.pallas_call(
+        k_all, v_all, pay, q_own, kn, vn = pl.pallas_call(
             first_kernel,
             out_shape=(pltpu.VMEM((n_seq, rows, head), bf16), pltpu.VMEM((n_seq, rows, head), bf16),
-                       payload, payload, payload,
-                       pltpu.VMEM((q4, n_q, head), f32), pltpu.VMEM((n_seq, 16, head), f32),
+                       payload,
+                       pltpu.VMEM((2 * q4, n_q, head), f32), pltpu.VMEM((n_seq, 16, head), f32),
                        pltpu.VMEM((n_seq, 16, head), f32)),
             in_specs=[hbm] * 6,
-            out_specs=(vm,) * 8,
+            out_specs=(vm,) * 6,
             scratch_shapes=[
                 pltpu.SMEM((n_seq,), jnp.int32),
                 pltpu.VMEM((n_seq, d_model), bf16),
                 pltpu.VMEM((d_model // 128, 128), bf16),
-                pltpu.VMEM((3 * kv_local // W_HEADS, d_model, W_HEADS * head), bf16),
+                pltpu.VMEM((w_chunks, d_model, W_HEADS * head), bf16),
                 pltpu.VMEM((n_seq, d_model), bf16),
                 pltpu.VMEM((6 * kv_local, n_seq, head), f32),
                 pltpu.VMEM((n_seq, n_q, head), f32),
                 pltpu.VMEM((n_seq, head), f32),
                 pltpu.VMEM((n_q, rows), jnp.int32),
                 pltpu.VMEM((2, PART, n_q, rows), f32),
-                dma((3,)), dma((3 * kv_local // W_HEADS,)), dma((slots,)), dma((slots,)),
-                dma((3 * kv_local // W_HEADS,)), dma((3 * kv_local // W_HEADS,)),
+                payload, payload,
+                dma((3,)), dma((w_chunks,)), dma((slots,)), dma((slots,)),
+                dma((w_chunks + 1,)), dma((w_chunks + 1,)),
             ],
             compiler_params=pltpu.CompilerParams(
                 collective_id=1, has_side_effects=True, vmem_limit_bytes=FIRST_VMEM * 1024 * 1024),
@@ -401,28 +458,41 @@
             name='first',
         )(*map(pin, (positions, hidden, norm_scale.reshape(d_model // 128, 128), w_qkv, k_rows, v_rows)))
 
-        got0 = lax.ppermute(pay0, 'sp', [(i, i ^ 2) for i in range(4)])
-        got1 = lax.ppermute(pay1, 'sp', [(i, 3 - i) for i in range(4)])
-        got2 = lax.ppermute(pay2, 'sp', [(i, i ^ 1) for i in range(4)])
-
-        k_upd, v_upd, mine, _, _ = pl.pallas_call(
+        got = lax.ppermute(pay, 'sp', [(i, i ^ 2) for i in range(4)])
+
+        k_part, v_part, mine, k_late, v_late = pl.pallas_call(
             second_kernel,
             out_shape=(jax.ShapeDtypeStruct((n_seq, rows, head), bf16),
-                       jax.ShapeDtypeStruct((n_seq, rows, head), bf16), payload,
-                       pltpu.VMEM((n_seq, rows, head), bf16), pltpu.VMEM((n_seq, rows, head), bf16)),
+                       jax.ShapeDtypeStruct((n_seq, rows, head), bf16), payload2, late, late),
             in_specs=[hbm, vm, vm, vm, vm, vm],
             out_specs=(hbm, hbm, vm, vm, vm),
-            input_output_aliases={4: 3, 5: 4},
             scratch_shapes=[
                 pltpu.SMEM((n_seq,), jnp.int32),
                 pltpu.VMEM((n_q, rows), jnp.int32),
                 pltpu.VMEM((2, PART, n_q, rows), f32),
-                dma((1,)), dma((2, 4)),
+                dma((1,)), dma((2, n_seq // PART)),
             ],
-            compiler_params=pltpu.CompilerParams(vmem_limit_bytes=FIRST_VMEM * 1024 * 1024),
+            compiler_params=pltpu.CompilerParams(vmem_limit_bytes=12 * 1024 * 1024),
             cost_estimate=pl.CostEstimate(flops=2 * 10**10, bytes_accessed=4 * 10**7, transcendentals=0),
             name='second',
-        )(pin(positions), q_own, kn, vn, k_all, v_all)
+        )(positions, q_own, kn, vn, k_all, v_all)
+
+        swap = [(i, i ^ 1) for i in range(4)]
+        sib_mine = lax.ppermute(mine, 'sp', swap)
+        sib_got = lax.ppermute(got, 'sp', swap)
+
+        k_upd, v_upd = pl.pallas_call(
+            third_kernel,
+            out_shape=(jax.ShapeDtypeStruct((n_seq, rows, head), bf16),
+                       jax.ShapeDtypeStruct((n_seq, rows, head), bf16)),
+            in_specs=[vm, vm, hbm, hbm],
+            out_specs=(hbm, hbm),
+            input_output_aliases={2: 0, 3: 1},
+            scratch_shapes=[dma((2, n_seq // PART))],
+            compiler_params=pltpu.CompilerParams(vmem_limit_bytes=12 * 1024 * 1024),
+            cost_estimate=pl.CostEstimate(flops=2 * 10**10, bytes_accessed=4 * 10**7, transcendentals=0),
+            name='third',
+        )(k_late, v_late, k_part, v_part)
 
         half_cols = d_model // 2
         cc = half_cols // OUT_CHUNKS
@@ -434,11 +504,11 @@
             out_specs=vm,
             scratch_shapes=[
                 pltpu.VMEM((w_out.shape[0], half_cols), bf16),
-                pltpu.VMEM((q4, n_q, head), f32),
-                pltpu.VMEM((q4, n_q, head), f32),
+                pltpu.VMEM((2 * q4, n_q, head), f32),
+                pltpu.VMEM((2, q4 + 1, n_q, head), f32),
                 pltpu.VMEM((2 * q4, n_q * head), bf16),
                 chunk, chunk, chunk, chunk, chunk, chunk,
-                dma((OUT_CHUNKS,)), dma((2,)),
+                dma((OUT_CHUNKS,)),
                 dma((OUT_CHUNKS,)), dma((OUT_CHUNKS,)),
                 dma((OUT_CHUNKS,)), dma((OUT_CHUNKS,)),
                 dma((OUT_CHUNKS,)), dma((OUT_CHUNKS,)),
@@ -447,7 +517,7 @@
             compiler_params=pltpu.CompilerParams(
                 collective_id=0, has_side_effects=True, vmem_limit_bytes=50 * 1024 * 1024),
             name='finish',
-        )(hidden, pin(w_out), mine, got0, got1, got2)
+        )(hidden, pin(w_out), mine, sib_mine, got, sib_got)
         return h_out, k_upd.reshape(k_cache.shape), v_upd.reshape(v_cache.shape)
 
     return jax.shard_map(

time: 39.7 us -> 37.4 us (0.942)
  Pallas kernels: 35.2 us -> 32.2 us
  starting transfers between devices: 2.74 us -> 3.59 us
    pallas_call x0 -> x1, Pallas kernels: none -> 2.15 us  [local_step(): pl.pallas_call(third_kernel, out_shape=(jax.ShapeDtypeStruct((n_seq, rows...]
    pallas_call x1, Pallas kernels: 15.8 us -> 13.6 us  [local_step(): pl.pallas_call(finish_kernel, out_shape=jax.ShapeDtypeStruct((n_seq, d_mo...]
    pallas_call x1, Pallas kernels: 6.86 us -> 5.32 us  [local_step(): pl.pallas_call(second_kernel, out_shape=(jax.ShapeDtypeStruct((n_seq, row...]
    pallas_call x1, Pallas kernels: 12.6 us -> 11.1 us  [local_step(): pl.pallas_call(first_kernel, out_shape=(pltpu.VMEM((n_seq, rows, head), b...]
    ppermute x3, starting transfers between devices: 2.74 us -> 3.59 us  [the longest x1 3.07 us: local_step(): got = lax.ppermute(pay, 'sp', [(i, i ^ 2) for i in range(4)])]
    unnamed x3 -> x5, local copies, waits for them, and re-layouts: 0.8 us -> 0.8 us
  transfers between devices with their start and end apart: 3 -> 3, of which waited for: 1 -> 0; matrix products, arithmetic and copies ran while one was open for 0% -> 0% of each run, Pallas kernels for 17% -> 20%
where the time goes in v5:
time: 37.4 us; the launch traced here: 37.3 us
  Pallas kernels  32.2 us (86%)
  starting transfers between devices  3.59 us (10%)
  local copies, waits for them, and re-layouts  0.8 us (2%)
  between operations  0.71 us (2%)
    pallas_call x1, Pallas kernels, local_step(): pl.pallas_call(finish_kernel, out_shape=jax.ShapeDtypeStruct((n_seq, d_mo...  13.6 us
    pallas_call x1, Pallas kernels, local_step(): pl.pallas_call(first_kernel, out_shape=(pltpu.VMEM((n_seq, rows, head), b...  11.1 us
    pallas_call x1, Pallas kernels, local_step(): pl.pallas_call(second_kernel, out_shape=(jax.ShapeDtypeStruct((n_seq, row...  5.32 us
    ppermute x1, starting transfers between devices, local_step(): got = lax.ppermute(pay, 'sp', [(i, i ^ 2) for i in range(4)])  3.07 us
    pallas_call x1, Pallas kernels, local_step(): pl.pallas_call(third_kernel, out_shape=(jax.ShapeDtypeStruct((n_seq, rows...  2.15 us
    unnamed x5, local copies, waits for them, and re-layouts  0.8 us
  transfers between devices with their start and end apart: 3, of which 0 were waited for; matrix products, arithmetic and copies ran while one was open for 0% of the time, Pallas kernels for 20%

profile of v5, /device:TPU:0, one launch (start us, length us, event | category | flops | bytes accessed | tf_op | source)
XLA Modules:
  0.0 37.3 jit_solution(7372609273449554637)
XLA Ops:
  0.6 0.0 copy-start.1
  0.6 11.1 %first.1 = (bf16[64,512,128]{2,1,0:T(8,128)(2,1)S(1)}, bf16[64,512,128]{2,1,0:T(8,128)(2,1)S(1)}, f32[17,16,128]{2,1,0:T(8,128)S(1)}, f32[32,16,128]{2,1,0:T(8,1...) custom-call(s32[64]{0:T(128)} %pos_hbm.3, bf16[64,4096]{1,0:T(8,128)(2,1)} %h_ref.1, ...), custom_call_target="tpu_custom_call" | custom-call | flops 20000000000 | bytes 40000000 | tf_op jit(solution)/shard_map/first/pallas_call | solution.py:432
  11.8 3.1 %collective-permute-start.1 = (f32[17,16,128]{2,1,0:T(8,128)S(1)}, f32[17,16,128]{2,1,0:T(8,128)S(1)}, u32[]{:S(2)}, u32[]{:S(2)}) collective-permute-start(f32[17,16,128]{2,1,0:T(8,128)S(1)} %get-tuple-element.22), channel_id=1, source_target_pairs={{0,2},{1,3},{2,0},{3,1},{4,6},{5,7},{6,4},{7,5}} | collective-permute-start | bytes 417800 | tf_op jit(solution)/shard_map/ppermute | solution.py:461
  14.8 0.0 copy-done.1
  14.8 5.3 %second.1 = (bf16[64,512,128]{2,1,0:T(8,128)(2,1)}, bf16[64,512,128]{2,1,0:T(8,128)(2,1)}, f32[33,16,128]{2,1,0:T(8,128)S(1)}, bf16[16,512,128]{2,1,0:T(8,128)(2,1)S(1)}, bf16[16,512,128]{2,1,0:T(8,128)(2,1)S(1)}) custom-call(s32[64]{0:T(128)S(1)} %copy-done.1, f32[32,16,128]{2,1,0:T(8,128)S(1)} %get-tuple-element.16.q_ref, ...), custom_call_target="tpu_custom_call" | custom-call | flops 20000000000 | bytes 40000000 | tf_op jit(solution)/shard_map/second/pallas_call | solution.py:463
  20.2 0.0 collective-permute-start
  20.2 0.0 collective-permute-done.1.got_ref
  20.2 0.5 %collective-permute-start.2 = (f32[17,16,128]{2,1,0:T(8,128)S(1)}, f32[17,16,128]{2,1,0:T(8,128)S(1)}, u32[]{:S(2)}, u32[]{:S(2)}) collective-permute-start(f32[17,16,128]{2,1,0:T(8,128)S(1)} %collective-permute-done.1.got_ref), channel_id=1, source_target_pairs={{0,1},{1,0},{2,3},{3,2},{4,5},{5,4},{6,7},{7,6}} | collective-permute-start | bytes 417800 | tf_op jit(solution)/shard_map/ppermute | solution.py:482
  20.7 0.0 copy-start
  20.7 2.1 %third.1 = (bf16[64,512,128]{2,1,0:T(8,128)(2,1)}, bf16[64,512,128]{2,1,0:T(8,128)(2,1)}) custom-call(bf16[16,512,128]{2,1,0:T(8,128)(2,1)S(1)} %get-tuple-element.23.k_late, bf16[16,512,128]{2,1,0:T(8,128)(2,1)S(1)} %get-tuple-element.24.v_late, bf16[64,512,128]{2,1,0:T(8,128)(2,1)} %get-tuple-element.25.k_in, ...), custom_call_target="tpu_custom_call", output_to_operand_aliasing={{0}: (2, {}), {1}: (3, {})} | custom-call | flops 20000000000 | bytes 40000000 | tf_op jit(solution)/shard_map/third/pallas_call | solution.py:484
  22.8 0.0 collective-permute-done.sib_ref
  22.9 0.0 collective-permute-done.2.sib_got_ref
  22.9 0.0 copy-done
  22.9 13.6 %finish.1 = bf16[64,4096]{1,0:T(8,128)(2,1)S(1)} custom-call(bf16[64,4096]{1,0:T(8,128)(2,1)S(1)} %copy-done, bf16[2048,4096]{1,0:T(8,128)(2,1)} %w_ref.3, f32[33,16,128]{2,1,0:T(8,128)S(1)} %get-tuple-element.21.mine_ref, f32[33,16,128]{2,1,0:T(8,128)S(1)} %collective-permute-done.sib_ref, f32[17,16,128]{2,1,0:T(8,128)S(1)} %collective-permute-done.1.got_ref, ...), custom_call_target="tpu_custom_call" | custom-call | tf_op jit(solution)/shard_map/finish/pallas_call | solution.py:500
  36.5 0.8 %copy.15 = bf16[64,4096]{1,0:T(8,128)(2,1)} copy(bf16[64,4096]{1,0:T(8,128)(2,1)S(1)} %finish.1) | data formatting | bytes 1048576
Async XLA Ops:
  0.6 14.2 %copy-start.1 = (s32[64]{0:T(128)S(1)}, s32[64]{0:T(128)}, u32[]{:S(2)}) copy-start(s32[64]{0:T(128)} %pos_hbm.3) | copy-start | bytes 772
  11.8 8.4 %collective-permute-start.1 = (f32[17,16,128]{2,1,0:T(8,128)S(1)}, f32[17,16,128]{2,1,0:T(8,128)S(1)}, u32[]{:S(2)}, u32[]{:S(2)}) collective-permute-start(f32[17,16,128]{2,1,0:T(8,128)S(1)} %get-tuple-element.22), channel_id=1, source_target_pairs={{0,2},{1,3},{2,0},{3,1},{4,6},{5,7},{6,4},{7,5}} | collective-permute-start | bytes 417800 | tf_op jit(solution)/shard_map/ppermute | solution.py:461
  20.2 2.7 %collective-permute-start = (f32[33,16,128]{2,1,0:T(8,128)S(1)}, f32[33,16,128]{2,1,0:T(8,128)S(1)}, u32[]{:S(2)}, u32[]{:S(2)}) collective-permute-start(f32[33,16,128]{2,1,0:T(8,128)S(1)} %get-tuple-element.21.mine_ref), channel_id=1, source_target_pairs={{0,1},{1,0},{2,3},{3,2},{4,5},{5,4},{6,7},{7,6}} | collective-permute-start | bytes 811016 | tf_op jit(solution)/shard_map/ppermute | solution.py:481
  20.2 2.7 %collective-permute-start.2 = (f32[17,16,128]{2,1,0:T(8,128)S(1)}, f32[17,16,128]{2,1,0:T(8,128)S(1)}, u32[]{:S(2)}, u32[]{:S(2)}) collective-permute-start(f32[17,16,128]{2,1,0:T(8,128)S(1)} %collective-permute-done.1.got_ref), channel_id=1, source_target_pairs={{0,1},{1,0},{2,3},{3,2},{4,5},{5,4},{6,7},{7,6}} | collective-permute-start | bytes 417800 | tf_op jit(solution)/shard_map/ppermute | solution.py:482
  20.7 2.2 %copy-start = (bf16[64,4096]{1,0:T(8,128)(2,1)S(1)}, bf16[64,4096]{1,0:T(8,128)(2,1)}, u32[]{:S(2)}) copy-start(bf16[64,4096]{1,0:T(8,128)(2,1)} %h_ref.1) | copy-start | bytes 1572868

commit v6 on v5

--- a/solution.py
+++ b/solution.py
@@ -9,10 +9,11 @@
 
 MESH = pl.DeviceIdType.MESH
 NEG = -1e30
-PV_LAG = 4
-W_HEADS = 4
+PV_LAG = 8
+W_SPLIT = (4, 4, 4)
 PART = 8
-EARLY_PARTS = 6
+EARLY_PARTS = 7
+DOTS = 8
 OUT_CHUNKS = 8
 LN_EPS = 1e-5
 FIRST_VMEM = 36
@@ -36,6 +37,7 @@
     tile = jnp.clip(p // per, 0, rows // 16 - 1)
     at = pl.ds(pl.multiple_of(tile * 16, 16), 16)
     hit = lax.broadcasted_iota(jnp.int32, (16, head), 0) // kv_local == p - tile * per
+    kn, vn = (jnp.concatenate([new[:kv_local]] * per, axis=0) for new in (kn, vn))
     k_ref[at_b, at, :] = jnp.where(hit, kn, k_ref[at_b, at, :].astype(jnp.float32)).astype(jnp.bfloat16)
     v_ref[at_b, at, :] = jnp.where(hit, vn, v_ref[at_b, at, :].astype(jnp.float32)).astype(jnp.bfloat16)
 
@@ -104,7 +106,9 @@
     n_seq, d_model = h_ref.shape
     rows = k_ref.shape[1]
     head = k_ref.shape[2]
-    w_chunks, _, w_cols = w_buf.shape
+    w_chunks = len(W_SPLIT)
+    half_heads = w_buf.shape[1] // head
+    first_head = [sum(W_SPLIT[:t]) for t in range(w_chunks + 1)]
     n_q = q_ref.shape[1]
     kv_local = n_q // 4
     sp = lax.axis_index('sp')
@@ -122,8 +126,9 @@
         cp.start()
 
     def w_copy(t):
-        at = pl.multiple_of((core * w_chunks + t) * w_cols, 128)
-        return pltpu.make_async_copy(w_ref.at[:, pl.ds(at, w_cols)], w_buf.at[t], w_sem.at[t])
+        at, width = first_head[t] * head, W_SPLIT[t] * head
+        src = pl.ds(pl.multiple_of(core * half_heads * head + at, 128), width)
+        return pltpu.make_async_copy(w_ref.at[:, src], w_buf.at[:, pl.ds(at, width)], w_sem.at[t])
 
     def c_copies(i):
         src = pl.ds(starts[i // per_slot] + (i % per_slot) * PART, PART)
@@ -173,7 +178,6 @@
             cen * rstd * scale_ref[i:i + 1, :].astype(jnp.float32)).astype(jnp.bfloat16)
     pl.semaphore_wait(barrier, 1)
 
-    heads = w_cols // head
     sends = []
     for t in range(w_chunks):
         w_copy(t).wait()
@@ -181,22 +185,26 @@
             for i in range(4 * per_slot):
                 for c in c_copies(i):
                     c.start(priority=1)
-        acc = jnp.dot(u_ref[...], w_buf[t], preferred_element_type=jnp.float32)
+        acc = jnp.dot(u_ref[...], w_buf[:, first_head[t] * head:first_head[t + 1] * head],
+                      preferred_element_type=jnp.float32)
         qkv = jnp.clip(acc.astype(jnp.bfloat16).astype(jnp.float32), -8.0, 8.0)
-        at = (core * w_chunks + t) * heads
-        for j in range(heads):
+        at = core * half_heads + first_head[t]
+        for j in range(W_SPLIT[t]):
             val = qkv[:, j * head:(j + 1) * head]
-            qkv_ref[at + j] = rope(val) if (t * heads + j) % 6 < 5 else val
-        block = qkv_ref.at[pl.ds(at, heads)]
+            qkv_ref[at + j] = rope(val) if (first_head[t] + j) % 6 < 5 else val
+        block = qkv_ref.at[pl.ds(at, W_SPLIT[t])]
         sends.append(pltpu.make_async_remote_copy(
             src_ref=block, dst_ref=block, send_sem=send_sem.at[t], recv_sem=recv_sem.at[t],
             device_id=sib, device_id_type=MESH))
         sends[t].start()
     for cp in sends:
         cp.wait_recv()
+    half_seq = n_seq // 2
+    far_half = pl.ds(pl.multiple_of(half_seq - starts[2], half_seq), half_seq)
+    own_half = pl.ds(starts[2], half_seq)
     for g in range(kv_local):
         for j in range(4):
-            q_ref[:, g * 4 + j, :] = qkv_ref[g * 6 + j]
+            q_ref[:, g * 4 + j, :] = qkv_ref[g * 6 + j, far_half]
 
     lane_id = lax.broadcasted_iota(jnp.int32, (n_q, 128), 1)
     pays = [out_pay, pay_ref]
@@ -213,10 +221,12 @@
             c.wait()
 
     def out_at(b, o, m, l):
-        if b < 2 * kv_local:
-            g, new_ref = b // 2, (kn_ref, vn_ref)[b % 2]
-            for r in range(16 // kv_local):
-                new_ref[:, r * kv_local + g, :] = qkv_ref[g * 6 + 4 + b % 2]
+        if b < 6 * kv_local:
+            g, kind = divmod(b, 6)
+            if kind < 4:
+                q_own[:, g * 4 + kind, :] = qkv_ref[b, own_half]
+            else:
+                (kn_ref, vn_ref)[kind - 4][:, g, :] = qkv_ref[b]
         slot = b // q4
         pays[slot][b % q4] = o
         stats[slot] = put_stats(stats[slot], lane_id, b % q4, m, l)
@@ -225,7 +235,7 @@
             pay_copy.start()
 
     parts = [list(range(i * PART, (i + 1) * PART)) for i in range(2 * per_slot)]
-    attend_parts(parts, arrive, lambda b: q_ref[seq(b)], lambda b: pos_ref[seq(b)] - base - 1,
+    attend_parts(parts, arrive, lambda b: q_ref[seq(b) - half_seq + starts[2]], lambda b: pos_ref[seq(b)] - base - 1,
                  k_ref, v_ref, idx_ref, s_ref, out_at)
 
     pay_copy.wait_recv()
@@ -237,7 +247,6 @@
     for i in range(q4):
         pay_ref[i] = (pay_ref[i] * jnp.broadcast_to(f0[:, i:i + 1], (n_q, 128))
                       + sib_pay[i] * jnp.broadcast_to(f1[:, i:i + 1], (n_q, 128)))
-    q_own[...] = q_ref[pl.ds(starts[2], 2 * q4)]
     for i in range(2 * per_slot, 4 * per_slot):
         arrive(i)
     for cp in sends + [pay_copy]:
@@ -333,12 +342,15 @@
     own_col = c * half_cols
     oth_col = (1 - c) * half_cols
 
+    wc = half_cols // DOTS
+    per_dot = OUT_CHUNKS // DOTS
+
     def w_copy(j):
         return pltpu.make_async_copy(
-            w_ref.at[:, pl.ds(pl.multiple_of(own_col + j * cc, 128), cc)],
-            w_buf.at[:, pl.ds(j * cc, cc)], w_sem.at[j])
-
-    for j in range(OUT_CHUNKS):
+            w_ref.at[:, pl.ds(pl.multiple_of(own_col + j * wc, 128), wc)],
+            w_buf.at[:, pl.ds(j * wc, wc)], w_sem.at[j])
+
+    for j in range(DOTS):
         w_copy(j).start()
 
     barrier = pltpu.get_barrier_semaphore()
@@ -368,13 +380,16 @@
         lhs[:, n * 128:(n + 1) * 128] = att[:, n, :].astype(jnp.bfloat16)
 
     y_copy, x_copy, d_copy, e_copy = [], [], [], []
-    for j in range(OUT_CHUNKS):
-        w_copy(j).wait()
-        part[j] = jnp.dot(lhs[...], w_buf[:, j * cc:(j + 1) * cc], preferred_element_type=jnp.float32)
-        if j == 0:
+    for t in range(DOTS):
+        w_copy(t).wait()
+        prod = jnp.dot(lhs[...], w_buf[:, t * wc:(t + 1) * wc], preferred_element_type=jnp.float32)
+        if t == 0:
             pl.semaphore_wait(barrier, 3)
-        y_copy.append(remote(part.at[j], y_in.at[j], ys_sem.at[j], yr_sem.at[j], yn))
-        y_copy[j].start()
+        for k in range(per_dot):
+            j = t * per_dot + k
+            part[j] = prod[:, k * cc:(k + 1) * cc]
+            y_copy.append(remote(part.at[j], y_in.at[j], ys_sem.at[j], yr_sem.at[j], yn))
+            y_copy[j].start()
 
     my_rows = pl.ds(pl.multiple_of(x * (2 * q4), 2 * q4), 2 * q4)
     xn_rows = pl.ds(pl.multiple_of((1 - x) * (2 * q4), 2 * q4), 2 * q4)
@@ -424,7 +439,7 @@
         v_rows = v_cache.reshape(n_seq, rows, head)
         slots = n_seq // PART
         late = pltpu.VMEM((n_seq - EARLY_PARTS * PART, rows, head), bf16)
-        w_chunks = 3 * kv_local // W_HEADS
+        w_chunks = len(W_SPLIT)
 
         def pin(a):
             return pltpu.with_memory_space_constraint(a, pltpu.HBM)
@@ -433,18 +448,18 @@
             first_kernel,
             out_shape=(pltpu.VMEM((n_seq, rows, head), bf16), pltpu.VMEM((n_seq, rows, head), bf16),
                        payload,
-                       pltpu.VMEM((2 * q4, n_q, head), f32), pltpu.VMEM((n_seq, 16, head), f32),
-                       pltpu.VMEM((n_seq, 16, head), f32)),
+                       pltpu.VMEM((2 * q4, n_q, head), f32), pltpu.VMEM((n_seq, 8, head), f32),
+                       pltpu.VMEM((n_seq, 8, head), f32)),
             in_specs=[hbm] * 6,
             out_specs=(vm,) * 6,
             scratch_shapes=[
                 pltpu.SMEM((n_seq,), jnp.int32),
                 pltpu.VMEM((n_seq, d_model), bf16),
                 pltpu.VMEM((d_model // 128, 128), bf16),
-                pltpu.VMEM((w_chunks, d_model, W_HEADS * head), bf16),
+                pltpu.VMEM((d_model, 3 * kv_local * head), bf16),
                 pltpu.VMEM((n_seq, d_model), bf16),
                 pltpu.VMEM((6 * kv_local, n_seq, head), f32),
-                pltpu.VMEM((n_seq, n_q, head), f32),
+                pltpu.VMEM((n_seq // 2, n_q, head), f32),
                 pltpu.VMEM((n_seq, head), f32),
                 pltpu.VMEM((n_q, rows), jnp.int32),
                 pltpu.VMEM((2, PART, n_q, rows), f32),
@@ -508,7 +523,7 @@
                 pltpu.VMEM((2, q4 + 1, n_q, head), f32),
                 pltpu.VMEM((2 * q4, n_q * head), bf16),
                 chunk, chunk, chunk, chunk, chunk, chunk,
-                dma((OUT_CHUNKS,)),
+                dma((DOTS,)),
                 dma((OUT_CHUNKS,)), dma((OUT_CHUNKS,)),
                 dma((OUT_CHUNKS,)), dma((OUT_CHUNKS,)),
                 dma((OUT_CHUNKS,)), dma((OUT_CHUNKS,)),

time: 37.4 us -> 36.7 us (0.981)
  Pallas kernels: 32.2 us -> 31.5 us
    pallas_call x1, Pallas kernels: 2.15 us -> 1.46 us  [local_step(): pl.pallas_call(third_kernel, out_shape=(jax.ShapeDtypeStruct((n_seq, rows...]
    pallas_call x1, Pallas kernels: 5.32 us -> 5.95 us  [local_step(): pl.pallas_call(second_kernel, out_shape=(jax.ShapeDtypeStruct((n_seq, row...]
    pallas_call x1, Pallas kernels: 11.1 us -> 10.5 us  [local_step(): pl.pallas_call(first_kernel, out_shape=(pltpu.VMEM((n_seq, rows, head), b...]
where the time goes in v6:
time: 36.7 us; the launch traced here: 36.6 us
  Pallas kernels  31.5 us (86%)
  starting transfers between devices  3.57 us (10%)
  local copies, waits for them, and re-layouts  0.8 us (2%)
  between operations  0.71 us (2%)
    pallas_call x1, Pallas kernels, local_step(): pl.pallas_call(finish_kernel, out_shape=jax.ShapeDtypeStruct((n_seq, d_mo...  13.6 us
    pallas_call x1, Pallas kernels, local_step(): pl.pallas_call(first_kernel, out_shape=(pltpu.VMEM((n_seq, rows, head), b...  10.5 us
    pallas_call x1, Pallas kernels, local_step(): pl.pallas_call(second_kernel, out_shape=(jax.ShapeDtypeStruct((n_seq, row...  5.95 us
    ppermute x1, starting transfers between devices, local_step(): got = lax.ppermute(pay, 'sp', [(i, i ^ 2) for i in range(4)])  3.06 us
    pallas_call x1, Pallas kernels, local_step(): pl.pallas_call(third_kernel, out_shape=(jax.ShapeDtypeStruct((n_seq, rows...  1.46 us
    unnamed x5, local copies, waits for them, and re-layouts  0.8 us
  transfers between devices with their start and end apart: 3, of which 0 were waited for; matrix products, arithmetic and copies ran while one was open for 0% of the time, Pallas kernels for 20%

profile of v6, /device:TPU:0, one launch (start us, length us, event | category | flops | bytes accessed | tf_op | source)
XLA Modules:
  0.0 36.6 jit_solution(1201451937026306832)
XLA Ops:
  0.6 0.0 copy-start.1
  0.6 10.5 %first.1 = (bf16[64,512,128]{2,1,0:T(8,128)(2,1)S(1)}, bf16[64,512,128]{2,1,0:T(8,128)(2,1)S(1)}, f32[17,16,128]{2,1,0:T(8,128)S(1)}, f32[32,16,128]{2,1,0:T(8,1...) custom-call(s32[64]{0:T(128)} %pos_hbm.3, bf16[64,4096]{1,0:T(8,128)(2,1)} %h_ref.1, ...), custom_call_target="tpu_custom_call" | custom-call | flops 20000000000 | bytes 40000000 | tf_op jit(solution)/shard_map/first/pallas_call | solution.py:447
  11.1 3.1 %collective-permute-start.1 = (f32[17,16,128]{2,1,0:T(8,128)S(1)}, f32[17,16,128]{2,1,0:T(8,128)S(1)}, u32[]{:S(2)}, u32[]{:S(2)}) collective-permute-start(f32[17,16,128]{2,1,0:T(8,128)S(1)} %get-tuple-element.22), channel_id=1, source_target_pairs={{0,2},{1,3},{2,0},{3,1},{4,6},{5,7},{6,4},{7,5}} | collective-permute-start | bytes 417800 | tf_op jit(solution)/shard_map/ppermute | solution.py:476
  14.2 0.0 copy-done.1
  14.2 6.0 %second.1 = (bf16[64,512,128]{2,1,0:T(8,128)(2,1)}, bf16[64,512,128]{2,1,0:T(8,128)(2,1)}, f32[33,16,128]{2,1,0:T(8,128)S(1)}, bf16[8,512,128]{2,1,0:T(8,128)(2,1)S(1)}, bf16[8,512,128]{2,1,0:T(8,128)(2,1)S(1)}) custom-call(s32[64]{0:T(128)S(1)} %copy-done.1, f32[32,16,128]{2,1,0:T(8,128)S(1)} %get-tuple-element.16.q_ref, ...), custom_call_target="tpu_custom_call" | custom-call | flops 20000000000 | bytes 40000000 | tf_op jit(solution)/shard_map/second/pallas_call | solution.py:478
  20.2 0.0 collective-permute-start
  20.2 0.0 collective-permute-done.1.got_ref
  20.2 0.5 %collective-permute-start.2 = (f32[17,16,128]{2,1,0:T(8,128)S(1)}, f32[17,16,128]{2,1,0:T(8,128)S(1)}, u32[]{:S(2)}, u32[]{:S(2)}) collective-permute-start(f32[17,16,128]{2,1,0:T(8,128)S(1)} %collective-permute-done.1.got_ref), channel_id=1, source_target_pairs={{0,1},{1,0},{2,3},{3,2},{4,5},{5,4},{6,7},{7,6}} | collective-permute-start | bytes 417800 | tf_op jit(solution)/shard_map/ppermute | solution.py:497
  20.7 0.0 copy-start
  20.7 1.5 %third.1 = (bf16[64,512,128]{2,1,0:T(8,128)(2,1)}, bf16[64,512,128]{2,1,0:T(8,128)(2,1)}) custom-call(bf16[8,512,128]{2,1,0:T(8,128)(2,1)S(1)} %get-tuple-element.23.k_late, bf16[8,512,128]{2,1,0:T(8,128)(2,1)S(1)} %get-tuple-element.24.v_late, bf16[64,512,128]{2,1,0:T(8,128)(2,1)} %get-tuple-element.25.k_in, ...), custom_call_target="tpu_custom_call", output_to_operand_aliasing={{0}: (2, {}), {1}: (3, {})} | custom-call | flops 20000000000 | bytes 40000000 | tf_op jit(solution)/shard_map/third/pallas_call | solution.py:499
  22.2 0.0 collective-permute-done.sib_ref
  22.2 0.0 collective-permute-done.2.sib_got_ref
  22.2 0.0 copy-done
  22.2 13.6 %finish.1 = bf16[64,4096]{1,0:T(8,128)(2,1)S(1)} custom-call(bf16[64,4096]{1,0:T(8,128)(2,1)S(1)} %copy-done, bf16[2048,4096]{1,0:T(8,128)(2,1)} %w_ref.3, f32[33,16,128]{2,1,0:T(8,128)S(1)} %get-tuple-element.21.mine_ref, f32[33,16,128]{2,1,0:T(8,128)S(1)} %collective-permute-done.sib_ref, f32[17,16,128]{2,1,0:T(8,128)S(1)} %collective-permute-done.1.got_ref, ...), custom_call_target="tpu_custom_call" | custom-call | tf_op jit(solution)/shard_map/finish/pallas_call | solution.py:515
  35.9 0.8 %copy.15 = bf16[64,4096]{1,0:T(8,128)(2,1)} copy(bf16[64,4096]{1,0:T(8,128)(2,1)S(1)} %finish.1) | data formatting | bytes 1048576
Async XLA Ops:
  0.6 13.6 %copy-start.1 = (s32[64]{0:T(128)S(1)}, s32[64]{0:T(128)}, u32[]{:S(2)}) copy-start(s32[64]{0:T(128)} %pos_hbm.3) | copy-start | bytes 772
  11.1 9.1 %collective-permute-start.1 = (f32[17,16,128]{2,1,0:T(8,128)S(1)}, f32[17,16,128]{2,1,0:T(8,128)S(1)}, u32[]{:S(2)}, u32[]{:S(2)}) collective-permute-start(f32[17,16,128]{2,1,0:T(8,128)S(1)} %get-tuple-element.22), channel_id=1, source_target_pairs={{0,2},{1,3},{2,0},{3,1},{4,6},{5,7},{6,4},{7,5}} | collective-permute-start | bytes 417800 | tf_op jit(solution)/shard_map/ppermute | solution.py:476
  20.2 2.0 %collective-permute-start = (f32[33,16,128]{2,1,0:T(8,128)S(1)}, f32[33,16,128]{2,1,0:T(8,128)S(1)}, u32[]{:S(2)}, u32[]{:S(2)}) collective-permute-start(f32[33,16,128]{2,1,0:T(8,128)S(1)} %get-tuple-element.21.mine_ref), channel_id=1, source_target_pairs={{0,1},{1,0},{2,3},{3,2},{4,5},{5,4},{6,7},{7,6}} | collective-permute-start | bytes 811016 | tf_op jit(solution)/shard_map/ppermute | solution.py:496
  20.2 2.0 %collective-permute-start.2 = (f32[17,16,128]{2,1,0:T(8,128)S(1)}, f32[17,16,128]{2,1,0:T(8,128)S(1)}, u32[]{:S(2)}, u32[]{:S(2)}) collective-permute-start(f32[17,16,128]{2,1,0:T(8,128)S(1)} %collective-permute-done.1.got_ref), channel_id=1, source_target_pairs={{0,1},{1,0},{2,3},{3,2},{4,5},{5,4},{6,7},{7,6}} | collective-permute-start | bytes 417800 | tf_op jit(solution)/shard_map/ppermute | solution.py:497
  20.7 1.5 %copy-start = (bf16[64,4096]{1,0:T(8,128)(2,1)S(1)}, bf16[64,4096]{1,0:T(8,128)(2,1)}, u32[]{:S(2)}) copy-start(bf16[64,4096]{1,0:T(8,128)(2,1)} %h_ref.1) | copy-start | bytes 1572868

commit v7 on v6

--- a/solution.py
+++ b/solution.py
@@ -197,14 +197,16 @@
             src_ref=block, dst_ref=block, send_sem=send_sem.at[t], recv_sem=recv_sem.at[t],
             device_id=sib, device_id_type=MESH))
         sends[t].start()
-    for cp in sends:
-        cp.wait_recv()
     half_seq = n_seq // 2
     far_half = pl.ds(pl.multiple_of(half_seq - starts[2], half_seq), half_seq)
     own_half = pl.ds(starts[2], half_seq)
-    for g in range(kv_local):
-        for j in range(4):
-            q_ref[:, g * 4 + j, :] = qkv_ref[g * 6 + j, far_half]
+    for t in range(w_chunks):
+        sends[t].wait_recv()
+        for j in range(first_head[t], first_head[t + 1]):
+            for at in (j, half_heads + j):
+                g, kind = divmod(at, 6)
+                if kind < 4:
+                    q_ref[:, g * 4 + kind, :] = qkv_ref[at, far_half]
 
     lane_id = lax.broadcasted_iota(jnp.int32, (n_q, 128), 1)
     pays = [out_pay, pay_ref]

time: 36.7 us -> 36.6 us (level)
  no operation moved by 1% of the time
where the time goes in v7:
time: 36.6 us; the launch traced here: 36.5 us
  Pallas kernels  31.4 us (86%)
  starting transfers between devices  3.57 us (10%)
  local copies, waits for them, and re-layouts  0.8 us (2%)
  between operations  0.71 us (2%)
    pallas_call x1, Pallas kernels, local_step(): pl.pallas_call(finish_kernel, out_shape=jax.ShapeDtypeStruct((n_seq, d_mo...  13.6 us
    pallas_call x1, Pallas kernels, local_step(): pl.pallas_call(first_kernel, out_shape=(pltpu.VMEM((n_seq, rows, head), b...  10.4 us
    pallas_call x1, Pallas kernels, local_step(): pl.pallas_call(second_kernel, out_shape=(jax.ShapeDtypeStruct((n_seq, row...  5.95 us
    ppermute x1, starting transfers between devices, local_step(): got = lax.ppermute(pay, 'sp', [(i, i ^ 2) for i in range(4)])  3.06 us
    pallas_call x1, Pallas kernels, local_step(): pl.pallas_call(third_kernel, out_shape=(jax.ShapeDtypeStruct((n_seq, rows...  1.46 us
    unnamed x5, local copies, waits for them, and re-layouts  0.8 us
  transfers between devices with their start and end apart: 3, of which 0 were waited for; matrix products, arithmetic and copies ran while one was open for 0% of the time, Pallas kernels for 20%

profile of v7, /device:TPU:0, one launch (start us, length us, event | category | flops | bytes accessed | tf_op | source)
XLA Modules:
  0.0 36.5 jit_solution(7153738775225283488)
XLA Ops:
  0.6 0.0 copy-start.1
  0.6 10.4 %first.1 = (bf16[64,512,128]{2,1,0:T(8,128)(2,1)S(1)}, bf16[64,512,128]{2,1,0:T(8,128)(2,1)S(1)}, f32[17,16,128]{2,1,0:T(8,128)S(1)}, f32[32,16,128]{2,1,0:T(8,1...) custom-call(s32[64]{0:T(128)} %pos_hbm.3, bf16[64,4096]{1,0:T(8,128)(2,1)} %h_ref.1, ...), custom_call_target="tpu_custom_call" | custom-call | flops 20000000000 | bytes 40000000 | tf_op jit(solution)/shard_map/first/pallas_call | solution.py:449
  11.0 3.1 %collective-permute-start.1 = (f32[17,16,128]{2,1,0:T(8,128)S(1)}, f32[17,16,128]{2,1,0:T(8,128)S(1)}, u32[]{:S(2)}, u32[]{:S(2)}) collective-permute-start(f32[17,16,128]{2,1,0:T(8,128)S(1)} %get-tuple-element.22), channel_id=1, source_target_pairs={{0,2},{1,3},{2,0},{3,1},{4,6},{5,7},{6,4},{7,5}} | collective-permute-start | bytes 417800 | tf_op jit(solution)/shard_map/ppermute | solution.py:478
  14.1 0.0 copy-done.1
  14.1 6.0 %second.1 = (bf16[64,512,128]{2,1,0:T(8,128)(2,1)}, bf16[64,512,128]{2,1,0:T(8,128)(2,1)}, f32[33,16,128]{2,1,0:T(8,128)S(1)}, bf16[8,512,128]{2,1,0:T(8,128)(2,1)S(1)}, bf16[8,512,128]{2,1,0:T(8,128)(2,1)S(1)}) custom-call(s32[64]{0:T(128)S(1)} %copy-done.1, f32[32,16,128]{2,1,0:T(8,128)S(1)} %get-tuple-element.16.q_ref, ...), custom_call_target="tpu_custom_call" | custom-call | flops 20000000000 | bytes 40000000 | tf_op jit(solution)/shard_map/second/pallas_call | solution.py:480
  20.1 0.0 collective-permute-start
  20.1 0.0 collective-permute-done.1.got_ref
  20.1 0.5 %collective-permute-start.2 = (f32[17,16,128]{2,1,0:T(8,128)S(1)}, f32[17,16,128]{2,1,0:T(8,128)S(1)}, u32[]{:S(2)}, u32[]{:S(2)}) collective-permute-start(f32[17,16,128]{2,1,0:T(8,128)S(1)} %collective-permute-done.1.got_ref), channel_id=1, source_target_pairs={{0,1},{1,0},{2,3},{3,2},{4,5},{5,4},{6,7},{7,6}} | collective-permute-start | bytes 417800 | tf_op jit(solution)/shard_map/ppermute | solution.py:499
  20.6 0.0 copy-start
  20.6 1.5 %third.1 = (bf16[64,512,128]{2,1,0:T(8,128)(2,1)}, bf16[64,512,128]{2,1,0:T(8,128)(2,1)}) custom-call(bf16[8,512,128]{2,1,0:T(8,128)(2,1)S(1)} %get-tuple-element.23.k_late, bf16[8,512,128]{2,1,0:T(8,128)(2,1)S(1)} %get-tuple-element.24.v_late, bf16[64,512,128]{2,1,0:T(8,128)(2,1)} %get-tuple-element.25.k_in, ...), custom_call_target="tpu_custom_call", output_to_operand_aliasing={{0}: (2, {}), {1}: (3, {})} | custom-call | flops 20000000000 | bytes 40000000 | tf_op jit(solution)/shard_map/third/pallas_call | solution.py:501
  22.1 0.0 collective-permute-done.sib_ref
  22.1 0.0 collective-permute-done.2.sib_got_ref
  22.1 0.0 copy-done
  22.1 13.6 %finish.1 = bf16[64,4096]{1,0:T(8,128)(2,1)S(1)} custom-call(bf16[64,4096]{1,0:T(8,128)(2,1)S(1)} %copy-done, bf16[2048,4096]{1,0:T(8,128)(2,1)} %w_ref.3, f32[33,16,128]{2,1,0:T(8,128)S(1)} %get-tuple-element.21.mine_ref, f32[33,16,128]{2,1,0:T(8,128)S(1)} %collective-permute-done.sib_ref, f32[17,16,128]{2,1,0:T(8,128)S(1)} %collective-permute-done.1.got_ref, ...), custom_call_target="tpu_custom_call" | custom-call | tf_op jit(solution)/shard_map/finish/pallas_call | solution.py:517
  35.7 0.8 %copy.15 = bf16[64,4096]{1,0:T(8,128)(2,1)} copy(bf16[64,4096]{1,0:T(8,128)(2,1)S(1)} %finish.1) | data formatting | bytes 1048576
Async XLA Ops:
  0.6 13.5 %copy-start.1 = (s32[64]{0:T(128)S(1)}, s32[64]{0:T(128)}, u32[]{:S(2)}) copy-start(s32[64]{0:T(128)} %pos_hbm.3) | copy-start | bytes 772
  11.0 9.1 %collective-permute-start.1 = (f32[17,16,128]{2,1,0:T(8,128)S(1)}, f32[17,16,128]{2,1,0:T(8,128)S(1)}, u32[]{:S(2)}, u32[]{:S(2)}) collective-permute-start(f32[17,16,128]{2,1,0:T(8,128)S(1)} %get-tuple-element.22), channel_id=1, source_target_pairs={{0,2},{1,3},{2,0},{3,1},{4,6},{5,7},{6,4},{7,5}} | collective-permute-start | bytes 417800 | tf_op jit(solution)/shard_map/ppermute | solution.py:478
  20.1 2.0 %collective-permute-start = (f32[33,16,128]{2,1,0:T(8,128)S(1)}, f32[33,16,128]{2,1,0:T(8,128)S(1)}, u32[]{:S(2)}, u32[]{:S(2)}) collective-permute-start(f32[33,16,128]{2,1,0:T(8,128)S(1)} %get-tuple-element.21.mine_ref), channel_id=1, source_target_pairs={{0,1},{1,0},{2,3},{3,2},{4,5},{5,4},{6,7},{7,6}} | collective-permute-start | bytes 811016 | tf_op jit(solution)/shard_map/ppermute | solution.py:498
  20.1 2.0 %collective-permute-start.2 = (f32[17,16,128]{2,1,0:T(8,128)S(1)}, f32[17,16,128]{2,1,0:T(8,128)S(1)}, u32[]{:S(2)}, u32[]{:S(2)}) collective-permute-start(f32[17,16,128]{2,1,0:T(8,128)S(1)} %collective-permute-done.1.got_ref), channel_id=1, source_target_pairs={{0,1},{1,0},{2,3},{3,2},{4,5},{5,4},{6,7},{7,6}} | collective-permute-start | bytes 417800 | tf_op jit(solution)/shard_map/ppermute | solution.py:499
  20.6 1.5 %copy-start = (bf16[64,4096]{1,0:T(8,128)(2,1)S(1)}, bf16[64,4096]{1,0:T(8,128)(2,1)}, u32[]{:S(2)}) copy-start(bf16[64,4096]{1,0:T(8,128)(2,1)} %h_ref.1) | copy-start | bytes 1572868

commit v8 on v7

--- a/solution.py
+++ b/solution.py
@@ -9,7 +9,7 @@
 
 MESH = pl.DeviceIdType.MESH
 NEG = -1e30
-PV_LAG = 8
+PV_LAG = 6
 W_SPLIT = (4, 4, 4)
 PART = 8
 EARLY_PARTS = 7

time: 36.6 us -> 36.6 us (level)
  no operation moved by 1% of the time
where the time goes in v8:
time: 36.6 us; the launch traced here: 36.5 us
  Pallas kernels  31.4 us (86%)
  starting transfers between devices  3.57 us (10%)
  local copies, waits for them, and re-layouts  0.8 us (2%)
  between operations  0.71 us (2%)
    pallas_call x1, Pallas kernels, local_step(): pl.pallas_call(finish_kernel, out_shape=jax.ShapeDtypeStruct((n_seq, d_mo...  13.6 us
    pallas_call x1, Pallas kernels, local_step(): pl.pallas_call(first_kernel, out_shape=(pltpu.VMEM((n_seq, rows, head), b...  10.4 us
    pallas_call x1, Pallas kernels, local_step(): pl.pallas_call(second_kernel, out_shape=(jax.ShapeDtypeStruct((n_seq, row...  5.95 us
    ppermute x1, starting transfers between devices, local_step(): got = lax.ppermute(pay, 'sp', [(i, i ^ 2) for i in range(4)])  3.06 us
    pallas_call x1, Pallas kernels, local_step(): pl.pallas_call(third_kernel, out_shape=(jax.ShapeDtypeStruct((n_seq, rows...  1.46 us
    unnamed x5, local copies, waits for them, and re-layouts  0.8 us
  transfers between devices with their start and end apart: 3, of which 0 were waited for; matrix products, arithmetic and copies ran while one was open for 0% of the time, Pallas kernels for 20%

profile of v8, /device:TPU:0, one launch (start us, length us, event | category | flops | bytes accessed | tf_op | source)
XLA Modules:
  0.0 36.5 jit_solution(17048791175742589191)
XLA Ops:
  0.6 0.0 copy-start.1
  0.6 10.4 %first.1 = (bf16[64,512,128]{2,1,0:T(8,128)(2,1)S(1)}, bf16[64,512,128]{2,1,0:T(8,128)(2,1)S(1)}, f32[17,16,128]{2,1,0:T(8,128)S(1)}, f32[32,16,128]{2,1,0:T(8,1...) custom-call(s32[64]{0:T(128)} %pos_hbm.3, bf16[64,4096]{1,0:T(8,128)(2,1)} %h_ref.1, ...), custom_call_target="tpu_custom_call" | custom-call | flops 20000000000 | bytes 40000000 | tf_op jit(solution)/shard_map/first/pallas_call | solution.py:449
  11.0 3.1 %collective-permute-start.1 = (f32[17,16,128]{2,1,0:T(8,128)S(1)}, f32[17,16,128]{2,1,0:T(8,128)S(1)}, u32[]{:S(2)}, u32[]{:S(2)}) collective-permute-start(f32[17,16,128]{2,1,0:T(8,128)S(1)} %get-tuple-element.22), channel_id=1, source_target_pairs={{0,2},{1,3},{2,0},{3,1},{4,6},{5,7},{6,4},{7,5}} | collective-permute-start | bytes 417800 | tf_op jit(solution)/shard_map/ppermute | solution.py:478
  14.1 0.0 copy-done.1
  14.1 6.0 %second.1 = (bf16[64,512,128]{2,1,0:T(8,128)(2,1)}, bf16[64,512,128]{2,1,0:T(8,128)(2,1)}, f32[33,16,128]{2,1,0:T(8,128)S(1)}, bf16[8,512,128]{2,1,0:T(8,128)(2,1)S(1)}, bf16[8,512,128]{2,1,0:T(8,128)(2,1)S(1)}) custom-call(s32[64]{0:T(128)S(1)} %copy-done.1, f32[32,16,128]{2,1,0:T(8,128)S(1)} %get-tuple-element.16.q_ref, ...), custom_call_target="tpu_custom_call" | custom-call | flops 20000000000 | bytes 40000000 | tf_op jit(solution)/shard_map/second/pallas_call | solution.py:480
  20.1 0.0 collective-permute-start
  20.1 0.0 collective-permute-done.1.got_ref
  20.1 0.5 %collective-permute-start.2 = (f32[17,16,128]{2,1,0:T(8,128)S(1)}, f32[17,16,128]{2,1,0:T(8,128)S(1)}, u32[]{:S(2)}, u32[]{:S(2)}) collective-permute-start(f32[17,16,128]{2,1,0:T(8,128)S(1)} %collective-permute-done.1.got_ref), channel_id=1, source_target_pairs={{0,1},{1,0},{2,3},{3,2},{4,5},{5,4},{6,7},{7,6}} | collective-permute-start | bytes 417800 | tf_op jit(solution)/shard_map/ppermute | solution.py:499
  20.6 0.0 copy-start
  20.6 1.5 %third.1 = (bf16[64,512,128]{2,1,0:T(8,128)(2,1)}, bf16[64,512,128]{2,1,0:T(8,128)(2,1)}) custom-call(bf16[8,512,128]{2,1,0:T(8,128)(2,1)S(1)} %get-tuple-element.23.k_late, bf16[8,512,128]{2,1,0:T(8,128)(2,1)S(1)} %get-tuple-element.24.v_late, bf16[64,512,128]{2,1,0:T(8,128)(2,1)} %get-tuple-element.25.k_in, ...), custom_call_target="tpu_custom_call", output_to_operand_aliasing={{0}: (2, {}), {1}: (3, {})} | custom-call | flops 20000000000 | bytes 40000000 | tf_op jit(solution)/shard_map/third/pallas_call | solution.py:501
  22.1 0.0 collective-permute-done.sib_ref
  22.1 0.0 collective-permute-done.2.sib_got_ref
  22.1 0.0 copy-done
  22.1 13.6 %finish.1 = bf16[64,4096]{1,0:T(8,128)(2,1)S(1)} custom-call(bf16[64,4096]{1,0:T(8,128)(2,1)S(1)} %copy-done, bf16[2048,4096]{1,0:T(8,128)(2,1)} %w_ref.3, f32[33,16,128]{2,1,0:T(8,128)S(1)} %get-tuple-element.21.mine_ref, f32[33,16,128]{2,1,0:T(8,128)S(1)} %collective-permute-done.sib_ref, f32[17,16,128]{2,1,0:T(8,128)S(1)} %collective-permute-done.1.got_ref, ...), custom_call_target="tpu_custom_call" | custom-call | tf_op jit(solution)/shard_map/finish/pallas_call | solution.py:517
  35.7 0.8 %copy.15 = bf16[64,4096]{1,0:T(8,128)(2,1)} copy(bf16[64,4096]{1,0:T(8,128)(2,1)S(1)} %finish.1) | data formatting | bytes 1048576
Async XLA Ops:
  0.6 13.5 %copy-start.1 = (s32[64]{0:T(128)S(1)}, s32[64]{0:T(128)}, u32[]{:S(2)}) copy-start(s32[64]{0:T(128)} %pos_hbm.3) | copy-start | bytes 772
  11.0 9.1 %collective-permute-start.1 = (f32[17,16,128]{2,1,0:T(8,128)S(1)}, f32[17,16,128]{2,1,0:T(8,128)S(1)}, u32[]{:S(2)}, u32[]{:S(2)}) collective-permute-start(f32[17,16,128]{2,1,0:T(8,128)S(1)} %get-tuple-element.22), channel_id=1, source_target_pairs={{0,2},{1,3},{2,0},{3,1},{4,6},{5,7},{6,4},{7,5}} | collective-permute-start | bytes 417800 | tf_op jit(solution)/shard_map/ppermute | solution.py:478
  20.1 2.0 %collective-permute-start = (f32[33,16,128]{2,1,0:T(8,128)S(1)}, f32[33,16,128]{2,1,0:T(8,128)S(1)}, u32[]{:S(2)}, u32[]{:S(2)}) collective-permute-start(f32[33,16,128]{2,1,0:T(8,128)S(1)} %get-tuple-element.21.mine_ref), channel_id=1, source_target_pairs={{0,1},{1,0},{2,3},{3,2},{4,5},{5,4},{6,7},{7,6}} | collective-permute-start | bytes 811016 | tf_op jit(solution)/shard_map/ppermute | solution.py:498
  20.1 2.0 %collective-permute-start.2 = (f32[17,16,128]{2,1,0:T(8,128)S(1)}, f32[17,16,128]{2,1,0:T(8,128)S(1)}, u32[]{:S(2)}, u32[]{:S(2)}) collective-permute-start(f32[17,16,128]{2,1,0:T(8,128)S(1)} %collective-permute-done.1.got_ref), channel_id=1, source_target_pairs={{0,1},{1,0},{2,3},{3,2},{4,5},{5,4},{6,7},{7,6}} | collective-permute-start | bytes 417800 | tf_op jit(solution)/shard_map/ppermute | solution.py:499
  20.6 1.5 %copy-start = (bf16[64,4096]{1,0:T(8,128)(2,1)S(1)}, bf16[64,4096]{1,0:T(8,128)(2,1)}, u32[]{:S(2)}) copy-start(bf16[64,4096]{1,0:T(8,128)(2,1)} %h_ref.1) | copy-start | bytes 1572868
